TPU v7x, 512 devices: a 8x2x16 block of a 8x16x16 slice. The times are simulated.
512 devices in a mesh: groups: 2 (over y), seq: 16 (over z), head: 8 (over x), dim: 2 (over core).
Axes of the slice: x: 8, y: 2, z: 16, core: 2. Of those that a mesh axis runs over, the one named last changes fastest.
The devices are a block of a 8x16x16 slice.
Arguments:
- query: bfloat16 [4, 16, 4096, 128], P('groups', 'head', 'seq'), parts along dimension 0, may hold values from -6 to 6
- key: bfloat16 [4, 16, 4096, 128], P('groups', 'head', 'seq'), parts along dimension 0, may hold values from -6 to 6
- value: bfloat16 [4, 16, 128, 4096], P('groups', 'head', 'dim', 'seq'), parts along dimension 0, may hold values from -6 to 6
- out_gate: bfloat16 [4, 16, 128, 4096], P('groups', 'head', 'dim', 'seq'), parts along dimension 0, may hold values from -6 to 6
- beta: float32 [4, 16, 4096], P('groups', 'head', 'seq'), parts along dimension 0, may hold values from 0.1 to 0.9
- log_decay: float32 [4, 16, 4096], P('groups', 'head', 'seq'), parts along dimension 0, may hold values from -1 to 0, as said below
- lengths: int32 [4, 16], P('groups', 'seq'), parts along dimension 0, may hold values from 128 to 256
- norm_gain: float32 [128], P('dim'), may hold values from 0.1 to 1.9
Outputs:
- output: bfloat16 [4, 16, 128, 4096], P('groups', 'head', 'dim', 'seq'), parts along dimension 0
There are 2 independent parts, one for each index of `groups`. A program takes and returns all parts, laid end to end along the dimension named above; an argument that names none is the same for every part. Nothing has to cross between parts.
Inputs may be any that keep to these rules, and one draw needn't show every extreme that they name: `log_decay`: negative.
All inputs are finite; a program needn't handle non-finite values.
Results may differ from a plain program's by a relative error of at most 0.001.
Values sent between devices are 32-bit elements; how exact they have to be, the bound alone decides.
No kernel may reach another device: no remote copies, remote signals or barrier semaphores. Data moves between devices by JAX's collectives and lax.ppermute only.
A program may use at most 64 MiB of HBM per device.

v0:
```python
import jax
import jax.numpy as jnp
from jax import lax
from jax.sharding import PartitionSpec as P

DV = 128
TILE = 64
WINDOW = 4


FULL_PREC = lax.Precision.HIGHEST


def passed_along(value, axis, steps):
    count = lax.axis_size(axis)
    leading, last = (max(0, -steps), min(count, count - steps))
    return lax.ppermute(value, axis, [(source, source + steps) for source in range(leading, last)])


def gathered_total(shard, axis):
    return lax.all_gather(shard, axis).sum(0)


def apply_map(left, right):
    return jnp.matmul(left, right, precision=FULL_PREC)


def unit_lower_inverse(coupling, identity):
    negated = -coupling
    inverse = identity + negated
    power_now = negated
    for level_num in range(coupling.shape[-1].bit_length() - 2):
        power_now = apply_map(power_now, power_now)
        inverse = inverse + apply_map(inverse, power_now)
    return inverse


def tile_terms(query_t, unit_t, value_t, eff_rate, eff_decay):
    tile_len = query_t.shape[-2]
    cumlog = jnp.cumsum(eff_decay, axis=-1)
    index_row = jnp.arange(tile_len)
    causal = index_row[:, None] >= index_row[None, :]
    before = index_row[:, None] > index_row[None, :]
    log_gap = cumlog[..., :, None] - cumlog[..., None, :]
    decays = jnp.where(causal, jnp.exp(jnp.where(causal, log_gap, 0.0)), 0.0)
    key_gram = jnp.einsum("...rd,...sd->...rs", unit_t, unit_t, precision=FULL_PREC)
    coupling = jnp.where(before, eff_rate[..., :, None] * decays * key_gram, 0.0)
    identity = jnp.eye(tile_len, dtype=coupling.dtype)
    right_side = jnp.concatenate(
        [
            jnp.swapaxes(value_t, -1, -2) * eff_rate[..., None],
            unit_t * (eff_rate * jnp.exp(cumlog))[..., None],
        ],
        axis=-1,
    )
    solved = apply_map(unit_lower_inverse(coupling, identity), right_side)
    val_width = value_t.shape[-2]
    fresh_vals = solved[..., :val_width]
    key_mix = solved[..., val_width:]
    scores = decays * jnp.einsum("...rd,...sd->...rs", query_t, unit_t, precision=FULL_PREC)
    tile_end = cumlog[..., -1]
    carried = unit_t * jnp.exp(tile_end[..., None] - cumlog)[..., None]
    key_eye = jnp.eye(unit_t.shape[-1], dtype=carried.dtype)
    tile_map = jnp.exp(tile_end)[..., None, None] * key_eye - jnp.einsum(
        "...rd,...re->...de", key_mix, carried, precision=FULL_PREC
    )
    tile_add = jnp.einsum("...rv,...rd->...vd", fresh_vals, carried, precision=FULL_PREC)
    return (fresh_vals, key_mix, scores, cumlog, tile_map, tile_add)


def tile_output(start_state, query_t, key_mix, fresh_vals, scores, cumlog):
    new_vals = fresh_vals - jnp.einsum(
        "...rd,...vd->...rv", key_mix, start_state, precision=FULL_PREC
    )
    direct_term = jnp.einsum(
        "...vd,...rd->...vr", start_state, query_t * jnp.exp(cumlog)[..., None], precision=FULL_PREC
    )
    return direct_term + jnp.einsum("...sv,...rs->...vr", new_vals, scores, precision=FULL_PREC)


def local(query, key, value, out_gate, beta, log_decay, lengths, norm_gain):
    seq_count, head_count, tokens_here, key_width = query.shape
    val_width = value.shape[2]
    tile_count = tokens_here // TILE
    live_mask = (jnp.arange(tokens_here)[None, :] < lengths).astype(jnp.float32)
    key_float = key.astype(jnp.float32)
    unit_key = key_float / jnp.sqrt(jnp.sum(key_float * key_float, axis=-1, keepdims=True) + 1e-06)
    eff_rate = beta * live_mask[:, None, :]
    eff_decay = log_decay * live_mask[:, None, :]
    query_t = query.astype(jnp.float32).reshape(seq_count, head_count, tile_count, TILE, key_width)
    unit_t = unit_key.reshape(seq_count, head_count, tile_count, TILE, key_width)
    value_t = value.astype(jnp.float32).reshape(seq_count, head_count, val_width, tile_count, TILE)
    value_t = value_t.transpose(0, 1, 3, 2, 4)
    rate_t = eff_rate.reshape(seq_count, head_count, tile_count, TILE)
    decay_t = eff_decay.reshape(seq_count, head_count, tile_count, TILE)
    fresh_vals, key_mix, scores, cumlog, tile_map, tile_add = tile_terms(
        query_t, unit_t, value_t, rate_t, decay_t
    )

    def advance(carried_pair, inputs):
        state_now, trans_now = carried_pair
        map_now, add_now = inputs
        return (
            (apply_map(state_now, map_now) + add_now, apply_map(trans_now, map_now)),
            (state_now, trans_now),
        )

    initial = (
        jnp.zeros((seq_count, head_count, val_width, key_width), jnp.float32),
        jnp.broadcast_to(
            jnp.eye(key_width, dtype=jnp.float32), (seq_count, head_count, key_width, key_width)
        ),
    )
    (block_end, block_map), (starts, prefix) = lax.scan(
        advance, initial, (jnp.moveaxis(tile_map, 2, 0), jnp.moveaxis(tile_add, 2, 0))
    )
    summed, product = passed_along((block_end, block_map), "seq", 1)
    level_total = WINDOW.bit_length() - 1
    for level_num in range(level_total):
        earlier, earlier_map = passed_along((summed, product), "seq", 2**level_num)
        summed = apply_map(earlier, product) + summed
        if level_num + 1 < level_total:
            product = apply_map(earlier_map, product)
    start_full = jnp.moveaxis(starts + apply_map(summed[None], prefix), 0, 2)
    raw_out = tile_output(start_full, query_t, key_mix, fresh_vals, scores, cumlog)
    raw_out = raw_out.transpose(0, 1, 3, 2, 4).reshape(
        seq_count, head_count, val_width, tokens_here
    )
    squares = jnp.sum(raw_out * raw_out, axis=2)
    total_sq = gathered_total(squares, "dim")
    inv_rms = lax.rsqrt(total_sq / DV + 1e-06)
    gated_out = (
        raw_out
        * inv_rms[:, :, None, :]
        * norm_gain[None, None, :, None]
        * jax.nn.silu(out_gate.astype(jnp.float32))
        * live_mask[:, None, None, :]
    )
    return gated_out.astype(jnp.bfloat16)


def solution(mesh):
    in_specs = (
        P("groups", "head", "seq", None),
        P("groups", "head", "seq", None),
        P("groups", "head", "dim", "seq"),
        P("groups", "head", "dim", "seq"),
        P("groups", "head", "seq"),
        P("groups", "head", "seq"),
        P("groups", "seq"),
        P("dim"),
    )
    out_specs = P("groups", "head", "dim", "seq")
    return jax.shard_map(local, mesh=mesh, in_specs=in_specs, out_specs=out_specs, check_vma=False)
```

profile of v0, /device:TPU:65, one launch (start us, length us, event | category | flops | bytes accessed | tf_op | source)
XLA Modules:
  0.0 99.4 jit_solution(3327364277936782554)
XLA Ops:
  0.1 0.6 copy-done.18
  0.8 1.2 %fusion.23 = f32[2,2,256]{2,1,0:T(2,128)S(1)} fusion(bf16[2,2,256,128]{3,2,1,0:T(8,128)(2,1)} %param.11), kind=kLoop, calls=%fused_computation.43 | loop fusion | flops 392192 | bytes 266240 | tf_op jit(solution)/shard_map/reduce_sum | solution.py:87
  2.1 0.6 copy-done.15
  3.0 0.9 reduce_window_sum.11
  3.9 0.2 slice_reduce_fusion
  4.1 0.6 exponential_bitcast_fusion
  4.7 0.6 fusion.46
  5.3 0.7 copy.34
  6.0 0.2 convert_divide_fusion
  6.2 0.2 broadcast_multiply_fusion
  6.4 1.0 fusion.16
  7.4 0.6 fusion.47
  8.1 0.6 fusion.48
  8.7 0.7 convolution_add_fusion.4
  9.4 0.6 fusion.49
  10.0 0.6 convolution_add_fusion.3
  10.7 0.6 fusion.50
  11.3 0.6 convolution_add_fusion.2
  12.0 0.6 fusion.51
  12.6 0.6 convolution_add_fusion.1
  13.3 0.2 copy-done.7
  13.5 0.1 copy.35
  13.7 0.2 multiply_bitcast_fusion
  13.9 0.6 convolution_add_fusion
  14.5 1.2 %fusion.19 = f32[2,2,4,64,192]{4,3,2,1,0:T(8,128)S(1)} fusion(f32[2,2,4,64,64]{4,3,2,1,0:T(8,128)S(1)} %convolution_add_fusion, f32[2,2,4,64,128]{4,3,2,1,0:T(8,128)S(1)} %broadcast_multiply_fusion, f32[2,2,4,64,64]{4,3,2,1,0:T(8,128)S(1)} %multiply_bitcast_fusion), kind=kOutput, calls=%fused_computation.37 | convolution fusion | flops 151191552 | bytes 1835008 | tf_op jit(solution)/shard_map/dot_general | solution.py:25
  15.8 1.1 %convolution_bitcast_fusion.5 = f32[4,2,2,64,128]{4,3,0,2,1:T(8,128)S(1)} fusion(f32[2,2,4,64,192]{4,3,2,1,0:T(8,128)S(1)} %fusion.19, f32[2,2,4,64,128]{4,3,2,1,0:T(8,128)S(1)} %bitcast.112, f32[2,2,4,64]{3,2,1,0:T(4,128)S(1)} %get-tuple-element.110), kind=kOutput, calls=%fused_computation.32 | convolution fusion | flops 100794368 | bytes 1581056 | tf_op jit(solution)/shard_map/...rv,...rd->...vd/dot_general | solution.py:67
  17.0 2.3 %fusion.11 = f32[4,2,2,128,128]{4,3,0,2,1:T(8,128)S(1)} fusion(f32[128,128]{1,0:T(8,128)S(1)} %copy-done.4, f32[4,2,2]{0,2,1:T(2,128)S(1)} %copy-done.14, f32[2,2,4,64,192]{4,3,2,1,0:T(8,128)S(1)} %fusion.19, f32[2,2,4,64,128]{4,3,2,1,0:T(8,128)S(1)} %bitcast.113, f32[2,2,4,64]{3,2,1,0:T(4,128)S(1)} %get-tuple-element.110), kind=kOutput, calls=%fused_computation.16 | convolution fusion | flops 201981952 | bytes 2172928 | tf_op jit(solution)/shard_map/...rd,...re->...de/dot_general | solution.py:64
  19.4 9.8 %while.17 = (s32[]{:T(128)}, f32[2,2,64,128]{3,2,1,0:T(8,128)S(1)}, f32[2,2,128,128]{2,3,1,0:T(8,128)S(1)}, f32[4,2,2,64,128]{4,3,0,2,1:T(8,128)}, f32[4,2,2,128...) while((s32[]{:T(128)}, f32[2,2,64,128]{3,2,1,0:T(8,128)S(1)}, ...), condition=%wide.region_3.4_spmd.clone, body=%wide.region_2.3_spmd.clone.sunk | while | flops 151093248 | bytes 3016315 | solution.py:114
  19.4 0.7 bitcast_dynamic-update-slice_fusion.4
  20.1 0.3 fusion.99
  20.4 0.7 bitcast_dynamic-update-slice_fusion.5
  21.2 0.6 convolution_bitcast_fusion.7
  21.8 0.7 bitcast_dynamic-update-slice_fusion.4
  22.5 0.3 fusion.99
  22.9 0.8 bitcast_dynamic-update-slice_fusion.5
  23.6 0.6 convolution_bitcast_fusion.7
  24.3 0.7 bitcast_dynamic-update-slice_fusion.4
  25.0 0.3 fusion.99
  25.4 0.7 bitcast_dynamic-update-slice_fusion.5
  26.1 0.6 convolution_bitcast_fusion.7
  26.8 0.7 bitcast_dynamic-update-slice_fusion.4
  27.4 0.3 fusion.99
  27.8 0.7 bitcast_dynamic-update-slice_fusion.5
  28.5 0.6 convolution_bitcast_fusion.7
  29.3 6.6 %collective-permute-start.2 = (f32[2,2,128,128]{3,2,1,0:T(8,128)S(1)}, f32[2,2,128,128]{3,2,1,0:T(8,128)S(1)}, u32[]{:S(2)}, u32[]{:S(2)}) collective-permute-start(f32[2,2,128,128]{3,2,1,0:T(8,128)S(1)} %copy.39), channel_id=1, source_target_pairs={{0,16},{16,32},{32,48},{48,64},{64,80},{80,96},{96,112},{112,128},... | collective-permute-start | bytes 786440 | tf_op jit(solution)/shard_map/ppermute | solution.py:17
  35.9 5.7 %collective-permute-start = (f32[2,2,64,128]{3,2,1,0:T(8,128)S(1)}, f32[2,2,64,128]{3,2,1,0:T(8,128)S(1)}, u32[]{:S(2)}, u32[]{:S(2)}) collective-permute-start(f32[2,2,64,128]{3,2,1,0:T(8,128)S(1)} %get-tuple-element.46), channel_id=1, source_target_pairs={{0,16},{16,32},{32,48},{48,64},{64,80},{80,96},{96,112},{112,128},... | collective-permute-start | bytes 393224 | tf_op jit(solution)/shard_map/ppermute | solution.py:17
  41.6 1.9 %collective-permute-done = f32[2,2,64,128]{3,2,1,0:T(8,128)S(1)} collective-permute-done((f32[2,2,64,128]{3,2,1,0:T(8,128)S(1)}, f32[2,2,64,128]{3,2,1,0:T(8,128)S(1)}, u32[]{:S(2)}, u32[]{:S(2)}) %collective-permute-start) | collective-permute-done | bytes 131104 | tf_op jit(solution)/shard_map/ppermute | solution.py:17
  43.6 5.7 %collective-permute-start.1 = (f32[2,2,64,128]{3,2,1,0:T(8,128)S(1)}, f32[2,2,64,128]{3,2,1,0:T(8,128)S(1)}, u32[]{:S(2)}, u32[]{:S(2)}) collective-permute-start(f32[2,2,64,128]{3,2,1,0:T(8,128)S(1)} %collective-permute-done), channel_id=1, source_target_pairs={{0,16},{16,32},{32,48},{48,64},{64,80},{80,96},{96,112},{112,128},... | collective-permute-start | bytes 393224 | tf_op jit(solution)/shard_map/ppermute | solution.py:17
  49.3 7.0 %collective-permute-start.4 = (f32[2,2,128,128]{3,2,1,0:T(8,128)S(1)}, f32[2,2,128,128]{3,2,1,0:T(8,128)S(1)}, u32[]{:S(2)}, u32[]{:S(2)}) collective-permute-start(f32[2,2,128,128]{3,2,1,0:T(8,128)S(1)} %collective-permute-done.2), channel_id=1, source_target_pairs={{0,16},{16,32},{32,48},{48,64},{64,80},{80,96},{96,112},{112,128},... | collective-permute-start | bytes 786440 | tf_op jit(solution)/shard_map/ppermute | solution.py:17
  56.3 0.6 fusion.17
  56.9 0.4 convolution_add_fusion.7
  57.3 9.3 %collective-permute-start.3 = (f32[2,2,64,128]{3,2,1,0:T(8,128)S(1)}, f32[2,2,64,128]{3,2,1,0:T(8,128)S(1)}, u32[]{:S(2)}, u32[]{:S(2)}) collective-permute-start(f32[2,2,64,128]{3,2,1,0:T(8,128)S(1)} %convolution_add_fusion.7), channel_id=1, source_target_pairs={{0,32},{16,48},{32,64},{48,80},{64,96},{80,112},{96,128},{112,144}... | collective-permute-start | bytes 393224 | tf_op jit(solution)/shard_map/ppermute | solution.py:17
  66.6 0.4 fusion.52
  67.0 1.5 %collective-permute-done.3 = f32[2,2,64,128]{3,2,1,0:T(8,128)S(1)} collective-permute-done((f32[2,2,64,128]{3,2,1,0:T(8,128)S(1)}, f32[2,2,64,128]{3,2,1,0:T(8,128)S(1)}, u32[]{:S(2)}, u32[]{:S(2)}) %collective-permute-start.3) | collective-permute-done | bytes 131104 | tf_op jit(solution)/shard_map/ppermute | solution.py:17
  68.5 0.4 fusion.18
  68.9 1.3 %fusion.14 = f32[2,2,4,64,128]{4,3,2,1,0:T(8,128)S(1)} fusion(f32[4,2,2,64,128]{4,3,0,2,1:T(8,128)S(1)} %copy-done.5, f32[2,2,64,128,1]{3,2,4,1,0:T(8,128)S(1)} %fusion.18, f32[4,2,2,128,128]{3,4,0,2,1:T(8,128)S(1)} %copy-done.1), kind=kOutput, calls=%fused_computation.28 | convolution fusion | flops 201457664 | bytes 2228224 | tf_op jit(solution)/shard_map/dot_general | solution.py:25
  70.1 1.0 %convolution_subtract_fusion = f32[2,2,4,64,64]{4,3,2,1,0:T(8,128)S(1)} fusion(f32[2,2,4,64,128]{4,3,2,1,0:T(8,128)S(1)} %fusion.14, f32[2,2,4,64,192]{4,3,2,1,0:T(8,128)S(1)} %fusion.19), kind=kOutput, calls=%fused_computation.25 | convolution fusion | flops 100728832 | bytes 1572864 | tf_op jit(solution)/shard_map/...rd,...vd->...rv/dot_general | solution.py:72
  71.2 1.0 %fusion.24 = f32[2,2,4,64,64]{4,3,2,1,0:T(8,128)S(1)} fusion(f32[2,2,4,64,128]{4,3,2,1,0:T(8,128)S(1)} %fusion.14, bf16[2,2,4,64,128]{4,3,2,1,0:T(8,128)(2,1)S(1)} %bitcast.117, f32[2,2,4,64]{3,2,1,0:T(4,128)S(1)} %copy-done.11), kind=kOutput, calls=%fused_computation.45 | convolution fusion | flops 100925440 | bytes 1052672 | tf_op jit(solution)/shard_map/...vd,...rd->...vr/dot_general | solution.py:75
  72.2 1.0 %multiply_reduce_fusion = (f32[2,2,4,64]{3,2,1,0:T(4,128)S(1)}, f32[2,2,64,4,64]{4,2,3,1,0:T(8,128)S(1)}) fusion(f32[2,2,4,64,64]{4,3,2,1,0:T(8,128)S(1)} %fusion.24, f32[2,2,4,64,64]{4,3,2,1,0:T(8,128)S(1)} %convolution_subtract_fusion, f32[2,2,4,64,64]{4,3,2,1,0:T(8,128)S(1)} %fusion.17), kind=kOutput, calls=%fused_computation.44 | convolution fusion | flops 50527232 | bytes 1052672 | tf_op jit(solution)/shard_map/...sv,...rs->...vr/dot_general | solution.py:78
  73.3 24.0 %all_gather.7 = f32[2,2,2,256]{3,2,1,0:T(2,128)S(1)} all-gather(f32[1,2,2,256]{3,2,1,0:T(2,128)S(1)} %all_gather.6), channel_id=1, replica_groups=mesh['groups'=2,'seq'=16,'head'=8,'dim'=2] {'dim'}, dimensions={0}, use_global_device_ids=true | all-gather | bytes 12288 | tf_op jit(solution)/shard_map/all_gather | solution.py:21
  97.3 0.3 copy.44
  97.7 0.3 reshape.118
  98.1 0.5 copy-done.8
  98.6 0.8 fusion.42
  (61 shorter events, 0.8 us)
Async XLA Ops:
  0.0 6.4 %copy-start.9 = (pred[64,64]{1,0:T(8,128)(4,1)}, pred[64,64]{1,0:T(8,128)(4,1)S(1)}, u32[]{:S(2)}) copy-start(pred[64,64]{1,0:T(8,128)(4,1)S(1)} %get-tuple-element.115) | copy-start | bytes 12292
  0.1 5.2 %copy-start.3 = (f32[128,128]{1,0:T(8,128)}, f32[128,128]{1,0:T(8,128)S(1)}, u32[]{:S(2)}) copy-start(f32[128,128]{1,0:T(8,128)S(1)} %fusion.43) | copy-start | bytes 196612
  0.1 0.7 copy-start.18
  0.8 1.3 %copy-start.12 = (f32[2,256]{1,0:T(2,128)}, f32[2,256]{1,0:T(2,128)S(1)}, u32[]{:S(2)}) copy-start(f32[2,256]{1,0:T(2,128)S(1)} %compare_convert_fusion) | copy-start | bytes 6148
  0.8 5.2 %copy-start = (bf16[2,2,256,128]{3,2,1,0:T(8,128)(2,1)S(1)}, bf16[2,2,256,128]{3,2,1,0:T(8,128)(2,1)}, u32[]{:S(2)}) copy-start(bf16[2,2,256,128]{3,2,1,0:T(8,128)(2,1)} %param.11) | copy-start | bytes 786436
  2.1 0.7 copy-start.15
  2.1 0.7 copy-start.16
  12.6 0.9 copy-start.7
  15.8 1.2 %copy-start.4 = (f32[128,128]{1,0:T(8,128)S(1)}, f32[128,128]{1,0:T(8,128)}, u32[]{:S(2)}) copy-start(f32[128,128]{1,0:T(8,128)} %copy-done.3) | copy-start | bytes 196612
  15.8 1.2 %copy-start.14 = (f32[4,2,2]{0,2,1:T(2,128)S(1)}, f32[4,2,2]{0,2,1:T(2,128)}, u32[]{:S(2)}) copy-start(f32[4,2,2]{0,2,1:T(2,128)} %exponential_bitcast_fusion) | copy-start | bytes 196
  17.0 2.3 %copy-start.6 = (f32[128,128]{0,1:T(8,128)S(1)}, f32[128,128]{0,1:T(8,128)}, u32[]{:S(2)}) copy-start(f32[128,128]{0,1:T(8,128)} %copy.34) | copy-start | bytes 196612
  29.2 27.2 %copy-start.2 = (bf16[2,2,256,128]{3,2,1,0:T(8,128)(2,1)S(1)}, bf16[2,2,256,128]{3,2,1,0:T(8,128)(2,1)}, u32[]{:S(2)}) copy-start(bf16[2,2,256,128]{3,2,1,0:T(8,128)(2,1)} %param.10) | copy-start | bytes 786436
  29.2 27.2 %copy-start.10 = (pred[64,64]{1,0:T(8,128)(4,1)S(1)}, pred[64,64]{1,0:T(8,128)(4,1)}, u32[]{:S(2)}) copy-start(pred[64,64]{1,0:T(8,128)(4,1)} %copy-done.9) | copy-start | bytes 12292
  29.3 20.0 %collective-permute-start.2 = (f32[2,2,128,128]{3,2,1,0:T(8,128)S(1)}, f32[2,2,128,128]{3,2,1,0:T(8,128)S(1)}, u32[]{:S(2)}, u32[]{:S(2)}) collective-permute-start(f32[2,2,128,128]{3,2,1,0:T(8,128)S(1)} %copy.39), channel_id=1, source_target_pairs={{0,16},{16,32},{32,48},{48,64},{64,80},{80,96},{96,112},{112,128},... | collective-permute-start | bytes 786440 | tf_op jit(solution)/shard_map/ppermute | solution.py:17
  35.9 7.7 %collective-permute-start = (f32[2,2,64,128]{3,2,1,0:T(8,128)S(1)}, f32[2,2,64,128]{3,2,1,0:T(8,128)S(1)}, u32[]{:S(2)}, u32[]{:S(2)}) collective-permute-start(f32[2,2,64,128]{3,2,1,0:T(8,128)S(1)} %get-tuple-element.46), channel_id=1, source_target_pairs={{0,16},{16,32},{32,48},{48,64},{64,80},{80,96},{96,112},{112,128},... | collective-permute-start | bytes 393224 | tf_op jit(solution)/shard_map/ppermute | solution.py:17
  43.6 13.3 %collective-permute-start.1 = (f32[2,2,64,128]{3,2,1,0:T(8,128)S(1)}, f32[2,2,64,128]{3,2,1,0:T(8,128)S(1)}, u32[]{:S(2)}, u32[]{:S(2)}) collective-permute-start(f32[2,2,64,128]{3,2,1,0:T(8,128)S(1)} %collective-permute-done), channel_id=1, source_target_pairs={{0,16},{16,32},{32,48},{48,64},{64,80},{80,96},{96,112},{112,128},... | collective-permute-start | bytes 393224 | tf_op jit(solution)/shard_map/ppermute | solution.py:17
  49.3 17.2 %collective-permute-start.4 = (f32[2,2,128,128]{3,2,1,0:T(8,128)S(1)}, f32[2,2,128,128]{3,2,1,0:T(8,128)S(1)}, u32[]{:S(2)}, u32[]{:S(2)}) collective-permute-start(f32[2,2,128,128]{3,2,1,0:T(8,128)S(1)} %collective-permute-done.2), channel_id=1, source_target_pairs={{0,16},{16,32},{32,48},{48,64},{64,80},{80,96},{96,112},{112,128},... | collective-permute-start | bytes 786440 | tf_op jit(solution)/shard_map/ppermute | solution.py:17
  56.9 12.0 %copy-start.1 = (f32[4,2,2,128,128]{3,4,0,2,1:T(8,128)S(1)}, f32[4,2,2,128,128]{3,4,0,2,1:T(8,128)}, u32[]{:S(2)}) copy-start(f32[4,2,2,128,128]{3,4,0,2,1:T(8,128)} %get-tuple-element.48) | copy-start | bytes 3145732
  57.3 11.2 %collective-permute-start.3 = (f32[2,2,64,128]{3,2,1,0:T(8,128)S(1)}, f32[2,2,64,128]{3,2,1,0:T(8,128)S(1)}, u32[]{:S(2)}, u32[]{:S(2)}) collective-permute-start(f32[2,2,64,128]{3,2,1,0:T(8,128)S(1)} %convolution_add_fusion.7), channel_id=1, source_target_pairs={{0,32},{16,48},{32,64},{48,80},{64,96},{80,112},{96,128},{112,144}... | collective-permute-start | bytes 393224 | tf_op jit(solution)/shard_map/ppermute | solution.py:17
  67.0 1.9 %copy-start.5 = (f32[4,2,2,64,128]{4,3,0,2,1:T(8,128)S(1)}, f32[4,2,2,64,128]{4,3,0,2,1:T(8,128)}, u32[]{:S(2)}) copy-start(f32[4,2,2,64,128]{4,3,0,2,1:T(8,128)} %get-tuple-element.45) | copy-start | bytes 1572868
  70.1 1.0 %copy-start.11 = (f32[2,2,4,64]{3,2,1,0:T(4,128)S(1)}, f32[2,2,4,64]{3,2,1,0:T(4,128)}, u32[]{:S(2)}) copy-start(f32[2,2,4,64]{3,2,1,0:T(4,128)} %get-tuple-element.108) | copy-start | bytes 12292
  97.7 0.9 copy-start.8
  97.7 0.9 copy-start.13
  97.7 0.9 copy-start.17
where the time goes:
time: 99.7 us; the launch traced here: 99.4 us
  starting transfers between devices  34.3 us (34%)
  blocking collectives  24 us (24%)
  matrix products  22 us (22%)
  local copies, waits for them, and re-layouts  7.92 us (8%)
  other arithmetic  7.05 us (7%)
  waiting for transfers between devices  3.43 us (3%)
    ppermute x5, starting transfers between devices, passed_along(): lax.ppermute(value, axis, [(source, source + steps) for source in range(l...  34.3 us
    all_gather x1, blocking collectives, gathered_total(): return lax.all_gather(shard, axis).sum(0)  24 us
    dot_general x23, matrix products, apply_map(): return jnp.matmul(left, right, precision=FULL_PREC)  13.9 us
    ppermute x5, waiting for transfers between devices, passed_along(): lax.ppermute(value, axis, [(source, source + steps) for source in range(l...  3.43 us
    dynamic_update_slice x4, local copies, waits for them, and re-layouts, local(): lax.scan(advance, initial, (jnp.moveaxis(tile_map, 2, 0), jnp.moveaxis(ti...  2.94 us
    dynamic_update_slice x4, other arithmetic, local(): lax.scan(advance, initial, (jnp.moveaxis(tile_map, 2, 0), jnp.moveaxis(ti...  2.73 us
    dot_general x1, matrix products, tile_terms(): jnp.einsum('...rd,...re->...de', key_mix, carried, precision=FULL_PREC)  2.33 us
    unnamed x38, local copies, waits for them, and re-layouts  2.16 us
  transfers between devices with their start and end apart: 5, of which 2 were waited for; matrix products, arithmetic and copies ran while one was open for 1% of the time, Pallas kernels for 0%

commit v1 on v0

v1 whole, which is shorter than its diff:
```python
import jax
import jax.numpy as jnp
from jax import lax
from jax.experimental import pallas as pl
from jax.experimental.pallas import tpu as pltpu
from jax.sharding import PartitionSpec as P

WINDOW = 4
F32 = jnp.float32
BF16 = jnp.bfloat16


def dot(left, right):
    return jnp.dot(left, right, preferred_element_type=F32)


def split(full):
    high = full.astype(BF16)
    return high, (full - high.astype(F32)).astype(BF16)


def stack_rows(rows):
    blank = jnp.zeros_like(rows[0])
    return jnp.concatenate(rows + [blank] * (-len(rows) % 8), axis=0)


def state_kernel(
    lengths, key, value, beta, log_decay, end_out, map_out, inv_out, fix_out, decay_out, keys_out, cum_out
):
    seqs, heads, tokens, width = key.shape
    val_width = value.shape[2]
    half = tokens // 2
    pairs = [(b, h) for b in range(seqs) for h in range(heads)]
    lane = lax.broadcasted_iota(jnp.int32, (1, tokens), 1)
    row = lax.broadcasted_iota(jnp.int32, (tokens, tokens), 0)
    col = lax.broadcasted_iota(jnp.int32, (tokens, tokens), 1)
    upto = row <= col
    before = row < col
    eye = (row == col).astype(F32)
    low_row = lax.broadcasted_iota(jnp.int32, (half, half), 0)
    low_col = lax.broadcasted_iota(jnp.int32, (half, half), 1)
    apart = low_row ^ low_col
    low_eye = (low_row == low_col).astype(F32)

    live = [lane < lengths[b, 0] for b, _ in pairs]
    decays = stack_rows([jnp.where(live[i], log_decay[b, pl.ds(h, 1), :], 0.0) for i, (b, h) in enumerate(pairs)])
    ones = upto.astype(BF16)
    part0 = decays.astype(BF16)
    rest = decays - part0.astype(F32)
    part1 = rest.astype(BF16)
    part2 = (rest - part1.astype(F32)).astype(BF16)
    cum = dot(part0, ones) + (dot(part1, ones) + dot(part2, ones))
    cum_out[...] = cum

    keys_t, norms, scaled, weights, cums = [], [], [], [], []
    for i, (b, h) in enumerate(pairs):
        key_t = key[b, h].T
        wide = key_t.astype(F32)
        squares = jnp.sum(wide * wide, axis=0, keepdims=True) + 1e-06
        norm = lax.rsqrt(squares)
        c = cum[i : i + 1]
        rate = beta[b, pl.ds(h, 1), :]
        shift = jnp.where(live[i], c + 0.5 * jnp.log(squares) - jnp.log(rate), 1e30)
        weight = jnp.where(live[i], rate * norm * jnp.exp(c[:, tokens - 1 :] - c), 0.0)
        keys_t.append(key_t)
        norms.append(norm)
        cums.append(c)
        scaled.append(shift)
        weights.append(weight)
    columns = stack_rows(scaled + weights).T
    count = len(pairs)

    couplings, lows = [], []
    for i, (b, h) in enumerate(pairs):
        decay = jnp.exp(jnp.where(upto, cums[i] - columns[:, i : i + 1], -1e30))
        decay_out[i] = decay
        gram = dot(key[b, h], keys_t[i])
        couplings.append(jnp.where(before, gram * decay * norms[i], 0.0))
        for s in (0, half):
            lows.append(couplings[i][s : s + half, s : s + half])

    steps = [jnp.where(apart < 4, low, 0.0).astype(BF16) for low in lows]
    twos = [dot(n, n) for n in steps]
    invs = [low_eye - n.astype(F32) + t - dot(n, t.astype(BF16)) for n, t in zip(steps, twos)]
    size = 4
    while size < half:
        narrow = [x.astype(BF16) for x in invs]
        links = [
            jnp.where((apart >= size) & (apart < 2 * size), low, 0.0).astype(BF16) for low in lows
        ]
        mids = [dot(x, c).astype(BF16) for x, c in zip(narrow, links)]
        invs = [x - dot(m, n) for x, m, n in zip(invs, mids, narrow)]
        size *= 2

    coarse = []
    for i in range(count):
        first, second = invs[2 * i].astype(BF16), invs[2 * i + 1].astype(BF16)
        mid = dot(first, couplings[i][:half, half:].astype(BF16)).astype(BF16)
        corner = -dot(mid, second)
        coarse.append(
            jnp.concatenate(
                [
                    jnp.concatenate([first, corner.astype(BF16)], axis=1),
                    jnp.concatenate([jnp.zeros_like(first), second], axis=1),
                ],
                axis=0,
            )
        )
    fixes = []
    for i in range(count):
        high, low = split(couplings[i])
        left = (eye - coarse[i].astype(F32)) - (dot(high, coarse[i]) + dot(low, coarse[i]))
        fixes.append(dot(coarse[i], left.astype(BF16)).astype(BF16))
    for i, (b, h) in enumerate(pairs):
        inv_out[i] = coarse[i]
        fix_out[i] = fixes[i]
        high, low = split(key[b, h].astype(F32) * columns[:, count + i : count + i + 1])
        mixed = dot(coarse[i], high) + (dot(coarse[i], low) + dot(fixes[i], high))
        mixed_high, mixed_low = split(mixed)
        key_high, key_low = split(keys_t[i].astype(F32) * (jnp.exp(cums[i]) * norms[i]))
        stacked = jnp.concatenate([value[b, h], key_high, key_low], axis=0)
        keys_out[i] = stacked
        main = dot(stacked, mixed_high)
        extra = dot(stacked[: val_width + width], mixed_low)
        end_out[b, h] = main[:val_width] + extra[:val_width]
        taken = main[val_width : val_width + width] + (main[val_width + width :] + extra[val_width:])
        whole = jnp.exp(cums[i][:, tokens - 1 :])
        map_out[b, h] = whole * eye[:width, :width] - taken


def output_kernel(query, key, inv, fix, decay, keys, cum, own_out, carry_out):
    seqs, heads, tokens, width = query.shape
    val_width = own_out.shape[2]
    for b in range(seqs):
        for h in range(heads):
            i = b * heads + h
            query_t = query[b, h].T
            scores = dot(key[b, h], query_t) * decay[i]
            high, low = split(scores)
            mixed = dot(inv[i], high) + (dot(inv[i], low) + dot(fix[i], high))
            mixed_high, mixed_low = split(mixed)
            stacked = keys[i]
            main = dot(stacked, mixed_high)
            extra = dot(stacked[: val_width + width], mixed_low)
            own_out[b, h] = main[:val_width] + extra[:val_width]
            taken = main[val_width : val_width + width] + (main[val_width + width :] + extra[val_width:])
            carry_out[b, h] = query_t.astype(F32) * jnp.exp(cum[i : i + 1]) - taken


def raw_kernel(own, carry, state, raw_out, square_out):
    seqs, heads = own.shape[:2]
    rows = []
    for b in range(seqs):
        for h in range(heads):
            raw = own[b, h] + jnp.dot(
                state[b, h], carry[b, h], precision=lax.Precision.HIGH, preferred_element_type=F32
            )
            raw_out[b, h] = raw
            rows.append(jnp.sum(raw * raw, axis=0, keepdims=True))
    square_out[...] = stack_rows(rows)


def gate_kernel(lengths, raw, squares, gate, gain, out):
    seqs, heads, val_width, tokens = raw.shape
    total = jnp.sum(squares[...], axis=0)
    scale = lax.rsqrt(total / (val_width * squares.shape[0]) + 1e-06)
    lane = lax.broadcasted_iota(jnp.int32, (1, tokens), 1)
    for b in range(seqs):
        live = lane < lengths[b, 0]
        for h in range(heads):
            i = b * heads + h
            opened = gate[b, h].astype(F32)
            opened = opened / (1.0 + jnp.exp(-opened))
            factor = jnp.where(live, scale[i : i + 1], 0.0)
            out[b, h] = (raw[b, h] * factor * (gain[...] * opened)).astype(BF16)


def vmem(count):
    return [pl.BlockSpec(memory_space=pltpu.VMEM)] * count


def call(body, outs, *operands, scalars=0):
    return pl.pallas_call(
        body,
        out_shape=outs,
        in_specs=[pl.BlockSpec(memory_space=pltpu.SMEM)] * scalars + vmem(len(operands) - scalars),
        out_specs=jax.tree.map(lambda _: pl.BlockSpec(memory_space=pltpu.VMEM), outs),
        compiler_params=pltpu.CompilerParams(vmem_limit_bytes=60 * 1024 * 1024),
    )(*operands)


def local(query, key, value, out_gate, beta, log_decay, lengths, norm_gain):
    seqs, heads, tokens, width = query.shape
    val_width = value.shape[2]
    count = seqs * heads
    shape = jax.ShapeDtypeStruct
    block_end, block_map, inverse, fix, decay, keys, cum = call(
        state_kernel,
        (
            shape((seqs, heads, val_width, width), F32),
            shape((seqs, heads, width, width), F32),
            shape((count, tokens, tokens), BF16),
            shape((count, tokens, tokens), BF16),
            shape((count, tokens, tokens), F32),
            shape((count, val_width + 2 * width, tokens), BF16),
            shape((count + -count % 8, tokens), F32),
        ),
        lengths,
        key,
        value,
        beta,
        log_decay,
        scalars=1,
    )
    devices = lax.axis_size("seq")
    moving = block_end
    state = None
    for hop in range(1, WINDOW + 1):
        moving = lax.ppermute(moving, "seq", [(s, s + 1) for s in range(hop - 1, devices - 1)])
        state = moving if state is None else state + moving
        if hop < WINDOW:
            moving = jnp.matmul(moving, block_map, precision=lax.Precision.HIGH)
    own, carry = call(
        output_kernel,
        (
            shape((seqs, heads, val_width, tokens), F32),
            shape((seqs, heads, width, tokens), F32),
        ),
        query,
        key,
        inverse,
        fix,
        decay,
        keys,
        cum,
    )
    raw, squares = call(
        raw_kernel,
        (
            shape((seqs, heads, val_width, tokens), F32),
            shape((count + -count % 8, tokens), F32),
        ),
        own,
        carry,
        state,
    )
    squares = lax.all_gather(squares, "dim")
    return call(
        gate_kernel,
        shape((seqs, heads, val_width, tokens), BF16),
        lengths,
        raw,
        squares,
        out_gate,
        norm_gain[:, None],
        scalars=1,
    )


def solution(mesh):
    in_specs = (
        P("groups", "head", "seq", None),
        P("groups", "head", "seq", None),
        P("groups", "head", "dim", "seq"),
        P("groups", "head", "dim", "seq"),
        P("groups", "head", "seq"),
        P("groups", "head", "seq"),
        P("groups", "seq"),
        P("dim"),
    )
    out_specs = P("groups", "head", "dim", "seq")
    return jax.shard_map(local, mesh=mesh, in_specs=in_specs, out_specs=out_specs, check_vma=False)
```

time: 99.7 us -> 74.4 us (0.75)
  the two profiles are of different devices: /device:TPU:65 before, /device:TPU:577 now
where the time goes in v1:
time: 74.4 us; the launch traced here: 74.1 us
  blocking collectives  27.1 us (36%)
  starting transfers between devices  19.1 us (26%)
  Pallas kernels  17 us (23%)
  waiting for transfers between devices  6.39 us (9%)
  local copies, waits for them, and re-layouts  2.05 us (3%)
  matrix products  1.75 us (2%)
    all_gather x1, blocking collectives, local(): squares = lax.all_gather(squares, 'dim')  27.1 us
    ppermute x4, starting transfers between devices, local(): lax.ppermute(moving, 'seq', [(s, s + 1) for s in range(hop - 1, devices -...  19.1 us
    pallas_call x4, Pallas kernels, call(): pl.pallas_call(body, out_shape=outs, in_specs=[pl.BlockSpec(memory_space=...  17 us
    ppermute x4, waiting for transfers between devices, local(): lax.ppermute(moving, 'seq', [(s, s + 1) for s in range(hop - 1, devices -...  6.39 us
    dot_general x3, matrix products, local(): moving = jnp.matmul(moving, block_map, precision=lax.Precision.HIGH)  1.75 us
  transfers between devices with their start and end apart: 4, of which 3 were waited for; matrix products, arithmetic and copies ran while one was open for 1% of the time, Pallas kernels for 7%

profile of v1, /device:TPU:577, one launch (start us, length us, event | category | flops | bytes accessed | tf_op | source)
XLA Modules:
  0.0 74.1 jit_solution(3828957421983056162)
XLA Ops:
  0.0 1.3 %copy.10.lengths = s32[2,1]{1,0:T(2,128)} copy(s32[2,1]{0,1:T(1,128)} %param.14) | data formatting | bytes 16 | tf_op args[6]
  1.3 7.6 %shard_map.82 = (f32[2,2,64,128]{3,2,1,0:T(8,128)}, f32[2,2,128,128]{3,2,1,0:T(8,128)}, bf16[4,256,256]{2,1,0:T(8,128)(2,1)}, bf16[4,256,256]{2,1,0:T(8,128)(2,1...) custom-call(s32[2,1]{1,0:T(2,128)} %copy.10.lengths, bf16[2,2,256,128]{3,2,1,0:T(8,128)(2,1)} %key.3, ...), custom_call_target="tpu_custom_call" | custom-call | tf_op jit(solution)/shard_map/pallas_call | solution.py:183
  8.9 5.7 %collective-permute-start = (f32[2,2,64,128]{3,2,1,0:T(8,128)}, f32[2,2,64,128]{3,2,1,0:T(8,128)S(1)}, u32[]{:S(2)}, u32[]{:S(2)}) collective-permute-start(f32[2,2,64,128]{3,2,1,0:T(8,128)} %get-tuple-element.23), channel_id=1, source_target_pairs={{0,16},{16,32},{32,48},{48,64},{64,80},{80,96},{96,112},{112,128},... | collective-permute-start | bytes 393224 | tf_op jit(solution)/shard_map/ppermute | solution.py:219
  14.6 2.5 %collective-permute-done = f32[2,2,64,128]{3,2,1,0:T(8,128)S(1)} collective-permute-done((f32[2,2,64,128]{3,2,1,0:T(8,128)}, f32[2,2,64,128]{3,2,1,0:T(8,128)S(1)}, u32[]{:S(2)}, u32[]{:S(2)}) %collective-permute-start) | collective-permute-done | bytes 131104 | tf_op jit(solution)/shard_map/ppermute | solution.py:219
  17.2 0.0 copy-start
  17.2 1.3 %fusion = f32[2,2,64,128]{3,2,1,0:T(8,128)S(1)} fusion(f32[2,2,64,128]{3,2,1,0:T(8,128)S(1)} %collective-permute-done, f32[2,2,128,128]{3,2,1,0:T(8,128)} %get-tuple-element.24), kind=kOutput, calls=%fused_computation.1 | convolution fusion | flops 25165824 | bytes 524288 | tf_op jit(solution)/shard_map/dot_general | solution.py:222
  18.4 7.0 %collective-permute-start.1 = (f32[2,2,64,128]{3,2,1,0:T(8,128)S(1)}, f32[2,2,64,128]{3,2,1,0:T(8,128)S(1)}, u32[]{:S(2)}, u32[]{:S(2)}) collective-permute-start(f32[2,2,64,128]{3,2,1,0:T(8,128)S(1)} %fusion), channel_id=1, source_target_pairs={{16,32},{32,48},{48,64},{64,80},{80,96},{96,112},{112,128},{128,14... | collective-permute-start | bytes 393224 | tf_op jit(solution)/shard_map/ppermute | solution.py:219
  25.4 1.9 %collective-permute-done.1 = f32[2,2,64,128]{3,2,1,0:T(8,128)S(1)} collective-permute-done((f32[2,2,64,128]{3,2,1,0:T(8,128)S(1)}, f32[2,2,64,128]{3,2,1,0:T(8,128)S(1)}, u32[]{:S(2)}, u32[]{:S(2)}) %collective-permute-start.1) | collective-permute-done | bytes 131104 | tf_op jit(solution)/shard_map/ppermute | solution.py:219
  27.3 0.0 copy-done
  27.3 0.2 fusion.1
  27.6 5.8 %collective-permute-start.2 = (f32[2,2,64,128]{3,2,1,0:T(8,128)S(1)}, f32[2,2,64,128]{3,2,1,0:T(8,128)S(1)}, u32[]{:S(2)}, u32[]{:S(2)}) collective-permute-start(f32[2,2,64,128]{3,2,1,0:T(8,128)S(1)} %fusion.1), channel_id=1, source_target_pairs={{32,48},{48,64},{64,80},{80,96},{96,112},{112,128},{128,144},{144,... | collective-permute-start | bytes 393224 | tf_op jit(solution)/shard_map/ppermute | solution.py:219
  33.4 1.9 %collective-permute-done.2 = f32[2,2,64,128]{3,2,1,0:T(8,128)S(1)} collective-permute-done((f32[2,2,64,128]{3,2,1,0:T(8,128)S(1)}, f32[2,2,64,128]{3,2,1,0:T(8,128)S(1)}, u32[]{:S(2)}, u32[]{:S(2)}) %collective-permute-start.2) | collective-permute-done | bytes 131104 | tf_op jit(solution)/shard_map/ppermute | solution.py:219
  35.3 0.2 fusion.2
  35.5 0.0 copy-start.1
  35.5 0.7 collective-permute-start.3
  36.2 0.0 copy-done.1
  36.2 0.7 copy.11.gain
  36.9 5.5 %shard_map.83 = (f32[2,2,64,256]{3,2,1,0:T(8,128)}, f32[2,2,128,256]{3,2,1,0:T(8,128)}) custom-call(bf16[2,2,256,128]{3,2,1,0:T(8,128)(2,1)} %query.1, bf16[2,2,256,128]{3,2,1,0:T(8,128)(2,1)} %key.3, bf16[4,256,256]{2,1,0:T(8,128)(2,1)} %get-tuple-element.16.inv, bf16[4,256,256]{2,1,0:T(8,128)(2,1)} %get-tuple-element.17.fix, ...), custom_call_target="tpu_custom_call" | custom-call | tf_op jit(solution)/shard_map/pallas_call | solution.py:183
  42.5 0.0 collective-permute-done.3
  42.5 0.7 add_add_fusion.state
  43.1 2.1 %shard_map.84 = (f32[2,2,64,256]{3,2,1,0:T(8,128)}, f32[8,256]{1,0:T(8,128)}) custom-call(f32[2,2,64,256]{3,2,1,0:T(8,128)} %get-tuple-element.21.own, f32[2,2,128,256]{3,2,1,0:T(8,128)} %get-tuple-element.22.carry, f32[2,2,64,128]{3,2,1,0:T(8,128)} %add_add_fusion.state), custom_call_target="tpu_custom_call" | custom-call | tf_op jit(solution)/shard_map/pallas_call | solution.py:183
  45.3 27.1 %all-gather = f32[16,256]{1,0:T(8,128)} all-gather(f32[8,256]{1,0:T(8,128)} %get-tuple-element.26), channel_id=2, replica_groups=mesh['groups'=2,'seq'=16,'head'=8,'dim'=2] {'dim'}, dimensions={0}, use_global_device_ids=true | all-gather | bytes 24576 | tf_op jit(solution)/shard_map/all_gather | solution.py:247
  72.3 1.8 %shard_map.85 = bf16[2,2,64,256]{3,2,1,0:T(8,128)(2,1)} custom-call(s32[2,1]{1,0:T(2,128)} %copy.10.lengths, f32[2,2,64,256]{3,2,1,0:T(8,128)} %get-tuple-element.25.raw, f32[2,8,256]{2,1,0:T(8,128)} %bitcast.8, bf16[2,2,64,256]{3,2,1,0:T(8,128)(2,1)} %gate.1, f32[64,1]{1,0:T(8,128)} %copy.11.gain), custom_call_target="tpu_custom_call" | custom-call | tf_op jit(solution)/shard_map/pallas_call | solution.py:183
Async XLA Ops:
  8.9 8.3 %collective-permute-start = (f32[2,2,64,128]{3,2,1,0:T(8,128)}, f32[2,2,64,128]{3,2,1,0:T(8,128)S(1)}, u32[]{:S(2)}, u32[]{:S(2)}) collective-permute-start(f32[2,2,64,128]{3,2,1,0:T(8,128)} %get-tuple-element.23), channel_id=1, source_target_pairs={{0,16},{16,32},{32,48},{48,64},{64,80},{80,96},{96,112},{112,128},... | collective-permute-start | bytes 393224 | tf_op jit(solution)/shard_map/ppermute | solution.py:219
  17.2 10.2 %copy-start = (f32[2,2,128,128]{3,2,1,0:T(8,128)S(1)}, f32[2,2,128,128]{3,2,1,0:T(8,128)}, u32[]{:S(2)}) copy-start(f32[2,2,128,128]{3,2,1,0:T(8,128)} %get-tuple-element.24) | copy-start | bytes 786436
  18.4 8.9 %collective-permute-start.1 = (f32[2,2,64,128]{3,2,1,0:T(8,128)S(1)}, f32[2,2,64,128]{3,2,1,0:T(8,128)S(1)}, u32[]{:S(2)}, u32[]{:S(2)}) collective-permute-start(f32[2,2,64,128]{3,2,1,0:T(8,128)S(1)} %fusion), channel_id=1, source_target_pairs={{16,32},{32,48},{48,64},{64,80},{80,96},{96,112},{112,128},{128,14... | collective-permute-start | bytes 393224 | tf_op jit(solution)/shard_map/ppermute | solution.py:219
  27.6 7.7 %collective-permute-start.2 = (f32[2,2,64,128]{3,2,1,0:T(8,128)S(1)}, f32[2,2,64,128]{3,2,1,0:T(8,128)S(1)}, u32[]{:S(2)}, u32[]{:S(2)}) collective-permute-start(f32[2,2,64,128]{3,2,1,0:T(8,128)S(1)} %fusion.1), channel_id=1, source_target_pairs={{32,48},{48,64},{64,80},{80,96},{96,112},{112,128},{128,144},{144,... | collective-permute-start | bytes 393224 | tf_op jit(solution)/shard_map/ppermute | solution.py:219
  35.5 0.7 copy-start.1
  35.5 6.9 %collective-permute-start.3 = (f32[2,2,64,128]{3,2,1,0:T(8,128)S(1)}, f32[2,2,64,128]{3,2,1,0:T(8,128)S(1)}, u32[]{:S(2)}, u32[]{:S(2)}) collective-permute-start(f32[2,2,64,128]{3,2,1,0:T(8,128)S(1)} %fusion.2), channel_id=1, source_target_pairs={{48,64},{64,80},{80,96},{96,112},{112,128},{128,144},{144,160},{16... | collective-permute-start | bytes 393224 | tf_op jit(solution)/shard_map/ppermute | solution.py:219

commit v2 on v1

v2 whole, which is shorter than its diff:
```python
import jax
import jax.numpy as jnp
from jax import lax
from jax.experimental import pallas as pl
from jax.experimental.pallas import tpu as pltpu
from jax.sharding import PartitionSpec as P

WINDOW = 4
F32 = jnp.float32
BF16 = jnp.bfloat16


def dot(left, right):
    return jnp.dot(left, right, preferred_element_type=F32)


def split(full):
    high = full.astype(BF16)
    return high, (full - high.astype(F32)).astype(BF16)


def stack_rows(rows):
    blank = jnp.zeros_like(rows[0])
    return jnp.concatenate(rows + [blank] * (-len(rows) % 8), axis=0)


def state_kernel(
    lengths_in,
    key_in,
    value_in,
    beta_in,
    log_decay_in,
    query_in,
    gate_in,
    gain_in,
    end_out,
    mix_out,
    inv_out,
    fix_out,
    decay_out,
    keys_out,
    cum_out,
    live_out,
    key,
    query_out,
    gate_out,
    gain_out,
    value,
    lengths,
    high_ref,
    low_ref,
    beta,
    log_decay,
    sems,
):
    sources = [lengths_in, log_decay_in, beta_in, key_in, value_in, query_in, gate_in, gain_in]
    places = [lengths, log_decay, beta, key, value, query_out, gate_out, gain_out]
    copies = [pltpu.make_async_copy(s, p, sems.at[n]) for n, (s, p) in enumerate(zip(sources, places))]
    for copy in copies:
        copy.start()
    seqs, heads, tokens, width = key.shape
    val_width = value.shape[2]
    half = tokens // 2
    pairs = [(b, h) for b in range(seqs) for h in range(heads)]
    count = len(pairs)
    lane = lax.broadcasted_iota(jnp.int32, (1, tokens), 1)
    row = lax.broadcasted_iota(jnp.int32, (tokens, tokens), 0)
    col = lax.broadcasted_iota(jnp.int32, (tokens, tokens), 1)
    ones = (row <= col).astype(BF16)
    low_row = lax.broadcasted_iota(jnp.int32, (half, half), 0)
    low_col = lax.broadcasted_iota(jnp.int32, (half, half), 1)
    apart = low_row ^ low_col
    low_eye = (low_row == low_col).astype(F32)
    wide_eye = jnp.concatenate([low_eye, jnp.zeros_like(low_eye)], axis=1)
    masks = [(apart < 4).astype(BF16)]
    size = 4
    while size < half:
        masks.append(((apart >= size) & (apart < 2 * size)).astype(BF16))
        size *= 2

    for copy in copies[:2]:
        copy.wait()
    live = [lane < lengths[0, b] for b, _ in pairs]
    live_out[...] = stack_rows([mask.astype(F32) for mask in live])
    decays = stack_rows([jnp.where(live[i], log_decay[b, pl.ds(h, 1), :], 0.0) for i, (b, h) in enumerate(pairs)])
    part0 = decays.astype(BF16)
    rest = decays - part0.astype(F32)
    part1 = rest.astype(BF16)
    part2 = (rest - part1.astype(F32)).astype(BF16)
    cum = dot(part0, ones) + (dot(part1, ones) + dot(part2, ones))
    cum_out[...] = cum

    for copy in copies[2:4]:
        copy.wait()
    keys_t, norms, shifts, weights, cums = [], [], [], [], []
    for i, (b, h) in enumerate(pairs):
        key_t = key[b, h].T
        wide = key_t.astype(F32)
        squares = jnp.sum(wide * wide, axis=0, keepdims=True) + 1e-06
        norm = lax.rsqrt(squares)
        c = cum[i : i + 1]
        rate = beta[b, pl.ds(h, 1), :]
        keys_t.append(key_t)
        norms.append(norm)
        cums.append(c)
        shifts.append(jnp.where(live[i], c + 0.5 * jnp.log(squares) - jnp.log(rate), 1e30))
        weights.append(jnp.where(live[i], rate * norm * jnp.exp(c[:, tokens - 1 :] - c), 0.0))
    columns = stack_rows(shifts + weights).T

    grams = [
        [
            dot(key[b, h, :half], keys_t[i]),
            dot(key[b, h, half:], keys_t[i][:, half:]),
        ]
        for i, (b, h) in enumerate(pairs)
    ]
    for i in range(count):
        shift = columns[:, i : i + 1]
        for r, c in ((0, 0), (0, half), (half, half)):
            gap = cums[i][:, c : c + half] - shift[r : r + half]
            if r == c:
                gap = jnp.where(low_row <= low_col, gap, -1e30)
            decay = jnp.exp(gap)
            decay_out[i, r : r + half, c : c + half] = decay
            gram = grams[i][1] if r else grams[i][0][:, c : c + half]
            link = gram * decay * norms[i][:, c : c + half]
            if r == c:
                link = jnp.where(low_row < low_col, link, 0.0)
            high, low = split(link)
            high_ref[i, r : r + half, c : c + half] = high
            low_ref[i, r : r + half, c : c + half] = low
        high_ref[i, half:, :half] = jnp.zeros((half, half), BF16)
        low_ref[i, half:, :half] = jnp.zeros((half, half), BF16)

    for copy in copies[4:]:
        copy.wait()
    members = range(count)
    blocks = [(i, s) for i in members for s in (0, half)]
    steps = [high_ref[i, s : s + half, s : s + half] * masks[0] for i, s in blocks]
    twos = [dot(n, n) for n in steps]
    invs = [(low_eye - n.astype(F32) + t - dot(n, t.astype(BF16))).astype(BF16) for n, t in zip(steps, twos)]
    for mask in masks[1:]:
        mids = [
            dot(x, high_ref[i, s : s + half, s : s + half] * mask).astype(BF16) for x, (i, s) in zip(invs, blocks)
        ]
        invs = [x - dot(m, x).astype(BF16) for x, m in zip(invs, mids)]
    mids = [dot(invs[2 * i], high_ref[i, :half, half:]).astype(BF16) for i in members]
    corners = [-dot(mid, invs[2 * i + 1]).astype(BF16) for i, mid in enumerate(mids)]
    for i in members:
        inv_out[i, :half, :half] = invs[2 * i]
        inv_out[i, :half, half:] = corners[i]
        inv_out[i, half:, :half] = jnp.zeros_like(corners[i])
        inv_out[i, half:, half:] = invs[2 * i + 1]
    sides = [split(key[pairs[i]].astype(F32) * columns[:, count + i : count + i + 1]) for i in members]
    tops = [
        dot(
            jnp.concatenate([inv_out[i, :half], inv_out[i, :half]], axis=1),
            jnp.concatenate([high_ref[i], low_ref[i]], axis=0),
        )
        for i in members
    ]
    bottoms = [
        dot(
            jnp.concatenate([invs[2 * i + 1], invs[2 * i + 1]], axis=1),
            jnp.concatenate([high_ref[i, half:, half:], low_ref[i, half:, half:]], axis=0),
        )
        for i in members
    ]
    mixes = [dot(inv_out[i], jnp.concatenate(sides[i], axis=1)) for i in members]
    for i in members:
        fix_out[i, :half] = (wide_eye - inv_out[i, :half].astype(F32) - tops[i]).astype(BF16)
        fix_out[i, half:, :half] = jnp.zeros((half, half), BF16)
        fix_out[i, half:, half:] = (low_eye - invs[2 * i + 1].astype(F32) - bottoms[i]).astype(BF16)
    mixes = [mixed[:, :width] + mixed[:, width:] for mixed in mixes]
    parts = [split(mixed + dot(fix_out[i], mixed.astype(BF16))) for i, mixed in enumerate(mixes)]
    for i, (high, low) in enumerate(parts):
        end_out[pairs[i]] = from_values_narrow(value[pairs[i]], high, low)
        mix_out[i, 0] = high
        mix_out[i, 1] = low
    for i in members:
        key_high, key_low = split(keys_t[i].astype(F32) * (jnp.exp(cums[i]) * norms[i]))
        keys_out[i, 0] = key_high
        keys_out[i, 1] = key_low


def from_values(value, high, low):
    return dot(jnp.concatenate([value, value], axis=1), jnp.concatenate([high, low], axis=0))


def from_values_narrow(value, high, low):
    both = dot(value, jnp.concatenate([high, low], axis=1))
    return both[:, : high.shape[1]] + both[:, high.shape[1] :]


def from_keys(key_high, key_low, high, low):
    return dot(
        jnp.concatenate([key_high, key_low, key_high], axis=1), jnp.concatenate([high, high, low], axis=0)
    )


def output_kernel(query, key, value, mix, inv, fix, decay, keys, cum, own_out, carry_out, map_out):
    seqs, heads, tokens, width = query.shape
    half = tokens // 2
    pairs = [(b, h) for b in range(seqs) for h in range(heads)]
    queries = [query[pair].T for pair in pairs]
    fixes = [dot(fix[i], inv[i]) for i in range(len(pairs))]
    tops = [dot(key[b, h, :half], query_t) for (b, h), query_t in zip(pairs, queries)]
    bottoms = [dot(key[b, h, half:], query_t[:, half:]) for (b, h), query_t in zip(pairs, queries)]
    parts = []
    for i, (top, bottom) in enumerate(zip(tops, bottoms)):
        bottom = bottom * decay[i, half:, half:]
        bottom = jnp.concatenate([jnp.zeros_like(bottom), bottom], axis=1)
        parts.append(split(jnp.concatenate([top * decay[i, :half], bottom], axis=0)))
    mixes = [
        dot(
            jnp.concatenate([inv[i], inv[i], fixes[i].astype(BF16)], axis=1),
            jnp.concatenate([high, low, high], axis=0),
        )
        for i, (high, low) in enumerate(parts)
    ]
    eye = (
        lax.broadcasted_iota(jnp.int32, (width, width), 0) == lax.broadcasted_iota(jnp.int32, (width, width), 1)
    ).astype(F32)
    for i, pair in enumerate(pairs):
        whole = jnp.exp(cum[i : i + 1, tokens - 1 :])
        both = from_values_narrow(keys[i, 0], mix[i, 0], mix[i, 1])
        map_out[pair] = whole * eye - (both + dot(keys[i, 1], mix[i, 0]))
    parts = [split(mixed) for mixed in mixes]
    for i, (high, low) in enumerate(parts):
        own_out[pairs[i]] = from_values(value[pairs[i]], high, low)
    for i, (high, low) in enumerate(parts):
        taken = from_keys(keys[i, 0], keys[i, 1], high, low)
        carry_out[pairs[i]] = queries[i].astype(F32) * jnp.exp(cum[i : i + 1]) - taken


def raw_kernel(own, carry, *rest):
    *states, raw_out, square_out = rest
    seqs, heads = own.shape[:2]
    rows = []
    for b in range(seqs):
        for h in range(heads):
            state = states[0][b, h]
            for arrived in states[1:]:
                state = state + arrived[b, h]
            raw = own[b, h] + jnp.dot(
                state, carry[b, h], precision=lax.Precision.HIGH, preferred_element_type=F32
            )
            raw_out[b, h] = raw
            rows.append(jnp.sum(raw * raw, axis=0, keepdims=True))
    square_out[...] = stack_rows(rows)


def gate_kernel(raw, squares, gate, gain, live, out):
    seqs, heads, val_width, tokens = raw.shape
    total = jnp.sum(squares[...], axis=0)
    scale = lax.rsqrt(total / (val_width * squares.shape[0]) + 1e-06)
    gains = jnp.broadcast_to(gain[...], (8, val_width)).T[:, :1]
    scale = scale * live[...]
    for b in range(seqs):
        for h in range(heads):
            i = b * heads + h
            opened = gate[b, h].astype(F32)
            opened = opened / (1.0 + jnp.exp(-opened))
            out[b, h] = (raw[b, h] * scale[i : i + 1] * (gains * opened)).astype(BF16)


VMEM = pl.BlockSpec(memory_space=pltpu.VMEM)


def call(body, outs, *operands, space=VMEM, scratch=()):
    return pl.pallas_call(
        body,
        out_shape=outs,
        in_specs=[space] * len(operands),
        out_specs=jax.tree.map(lambda _: VMEM, outs),
        scratch_shapes=scratch,
        compiler_params=pltpu.CompilerParams(vmem_limit_bytes=16 * 1024 * 1024),
    )(*operands)


def local(query, key, value, out_gate, beta, log_decay, lengths, norm_gain):
    seqs, heads, tokens, width = query.shape
    val_width = value.shape[2]
    count = seqs * heads
    shape = jax.ShapeDtypeStruct
    rows = shape((count + -count % 8, tokens), F32)
    lengths = lengths.T
    norm_gain = norm_gain[None, :]
    block_end, mix, inverse, fix, decay, keys, cum, live, key, query, out_gate, norm_gain, value = call(
        state_kernel,
        (
            shape((seqs, heads, val_width, width), F32),
            shape((count, 2, tokens, width), BF16),
            shape((count, tokens, tokens), BF16),
            shape((count, tokens, tokens), BF16),
            shape((count, tokens, tokens), F32),
            shape((count, 2, width, tokens), BF16),
            rows,
            rows,
            shape(key.shape, BF16),
            shape(query.shape, BF16),
            shape(out_gate.shape, BF16),
            shape(norm_gain.shape, F32),
            shape(value.shape, BF16),
        ),
        *[
            pltpu.with_memory_space_constraint(array, pltpu.HBM)
            for array in (lengths, key, value, beta, log_decay, query, out_gate, norm_gain)
        ],
        space=pl.BlockSpec(memory_space=pltpu.HBM),
        scratch=[
            pltpu.SMEM(lengths.shape, jnp.int32),
            pltpu.VMEM((count, tokens, tokens), BF16),
            pltpu.VMEM((count, tokens, tokens), BF16),
            pltpu.VMEM(beta.shape, F32),
            pltpu.VMEM(log_decay.shape, F32),
            pltpu.SemaphoreType.DMA((8,)),
        ],
    )
    steps = lax.axis_size("seq") - 1
    arrived = [lax.ppermute(block_end, "seq", [(s, s + 1) for s in range(steps)])]
    own, carry, block_map = call(
        output_kernel,
        (
            shape((seqs, heads, val_width, tokens), F32),
            shape((seqs, heads, width, tokens), F32),
            shape((seqs, heads, width, width), F32),
        ),
        query,
        key,
        value,
        mix,
        inverse,
        fix,
        decay,
        keys,
        cum,
    )
    for hop in range(1, WINDOW):
        moving = jnp.matmul(arrived[-1], block_map, precision=lax.Precision.HIGH)
        arrived.append(lax.ppermute(moving, "seq", [(s, s + 1) for s in range(hop, steps)]))
    raw, squares = call(
        raw_kernel,
        (shape((seqs, heads, val_width, tokens), F32), rows),
        own,
        carry,
        *arrived,
    )
    squares = lax.all_gather(squares, "dim")
    return call(
        gate_kernel,
        shape((seqs, heads, val_width, tokens), BF16),
        raw,
        squares,
        out_gate,
        norm_gain,
        live,
    )


def solution(mesh):
    in_specs = (
        P("groups", "head", "seq", None),
        P("groups", "head", "seq", None),
        P("groups", "head", "dim", "seq"),
        P("groups", "head", "dim", "seq"),
        P("groups", "head", "seq"),
        P("groups", "head", "seq"),
        P("groups", "seq"),
        P("dim"),
    )
    out_specs = P("groups", "head", "dim", "seq")
    return jax.shard_map(local, mesh=mesh, in_specs=in_specs, out_specs=out_specs, check_vma=False)
```

time: 74.4 us -> 59 us (0.79)
  the two profiles are of different devices: /device:TPU:577 before, /device:TPU:833 now
where the time goes in v2:
time: 59 us; the launch traced here: 58.8 us
  starting transfers between devices  24.3 us (41%)
  blocking collectives  20.2 us (34%)
  Pallas kernels  7.05 us (12%)
  waiting for transfers between devices  6.42 us (11%)
  matrix products  0.72 us (1%)
    all_gather x1, blocking collectives, local(): squares = lax.all_gather(squares, 'dim')  20.2 us
    ppermute x3, starting transfers between devices, local(): lax.ppermute(moving, 'seq', [(s, s + 1) for s in range(hop, steps)])  17.3 us
    pallas_call x4, Pallas kernels, call(): pl.pallas_call(body, out_shape=outs, in_specs=[space] * len(operands), ou...  7.05 us
    ppermute x1, starting transfers between devices, local(): lax.ppermute(block_end, 'seq', [(s, s + 1) for s in range(steps)])  6.96 us
    ppermute x3, waiting for transfers between devices, local(): lax.ppermute(moving, 'seq', [(s, s + 1) for s in range(hop, steps)])  5.77 us
  transfers between devices with their start and end apart: 4, of which 4 were waited for; matrix products, arithmetic and copies ran while one was open for 0% of the time, Pallas kernels for 3%

profile of v2, /device:TPU:833, one launch (start us, length us, event | category | flops | bytes accessed | tf_op | source)
XLA Modules:
  0.0 58.8 jit_solution(8638093615047010363)
XLA Ops:
  0.0 4.4 %shard_map.82 = (f32[2,2,64,128]{3,2,1,0:T(8,128)S(1)}, bf16[4,2,256,128]{3,2,1,0:T(8,128)(2,1)S(1)}, bf16[4,256,256]{2,1,0:T(8,128)(2,1)S(1)}, bf16[4,256,256]{...) custom-call(s32[1,2]{1,0:T(1,128)} %bitcast.10, ...), custom_call_target="tpu_custom_call" | custom-call | tf_op jit(solution)/shard_map/pallas_call | solution.py:271
  4.4 7.0 %collective-permute-start = (f32[2,2,64,128]{3,2,1,0:T(8,128)S(1)}, f32[2,2,64,128]{3,2,1,0:T(8,128)S(1)}, u32[]{:S(2)}, u32[]{:S(2)}) collective-permute-start(f32[2,2,64,128]{3,2,1,0:T(8,128)S(1)} %get-tuple-element.34), channel_id=1, source_target_pairs={{0,16},{16,32},{32,48},{48,64},{64,80},{80,96},{96,112},{112,128},... | collective-permute-start | bytes 393224 | tf_op jit(solution)/shard_map/ppermute | solution.py:321
  11.4 1.5 %shard_map.83 = (f32[2,2,64,256]{3,2,1,0:T(8,128)S(1)}, f32[2,2,128,256]{3,2,1,0:T(8,128)S(1)}, f32[2,2,128,128]{3,2,1,0:T(8,128)S(1)}) custom-call(bf16[2,2,256,128]{3,2,1,0:T(8,128)(2,1)S(1)} %get-tuple-element.23.query, bf16[2,2,256,128]{3,2,1,0:T(8,128)(2,1)S(1)} %get-tuple-element.24.key, bf16[2,2,64,256]{3,2,1,0:T(8,128)(2,1)S(1)} %get-tuple-element.25.value, ...), custom_call_target="tpu_custom_call" | custom-call | tf_op jit(solution)/shard_map/pallas_call | solution.py:271
  12.9 0.6 %collective-permute-done.rest_0_ = f32[2,2,64,128]{3,2,1,0:T(8,128)S(1)} collective-permute-done((f32[2,2,64,128]{3,2,1,0:T(8,128)S(1)}, f32[2,2,64,128]{3,2,1,0:T(8,128)S(1)}, u32[]{:S(2)}, u32[]{:S(2)}) %collective-permute-start) | collective-permute-done | bytes 131104 | tf_op jit(solution)/shard_map/ppermute | solution.py:321
  13.6 0.2 fusion
  13.8 5.8 %collective-permute-start.1 = (f32[2,2,64,128]{3,2,1,0:T(8,128)S(1)}, f32[2,2,64,128]{3,2,1,0:T(8,128)S(1)}, u32[]{:S(2)}, u32[]{:S(2)}) collective-permute-start(f32[2,2,64,128]{3,2,1,0:T(8,128)S(1)} %fusion), channel_id=1, source_target_pairs={{16,32},{32,48},{48,64},{64,80},{80,96},{96,112},{112,128},{128,14... | collective-permute-start | bytes 393224 | tf_op jit(solution)/shard_map/ppermute | solution.py:341
  19.6 1.9 %collective-permute-done.1.rest_1_ = f32[2,2,64,128]{3,2,1,0:T(8,128)S(1)} collective-permute-done((f32[2,2,64,128]{3,2,1,0:T(8,128)S(1)}, f32[2,2,64,128]{3,2,1,0:T(8,128)S(1)}, u32[]{:S(2)}, u32[]{:S(2)}) %collective-permute-start.1) | collective-permute-done | bytes 131104 | tf_op jit(solution)/shard_map/ppermute | solution.py:341
  21.6 0.2 fusion.1
  21.8 5.8 %collective-permute-start.2 = (f32[2,2,64,128]{3,2,1,0:T(8,128)S(1)}, f32[2,2,64,128]{3,2,1,0:T(8,128)S(1)}, u32[]{:S(2)}, u32[]{:S(2)}) collective-permute-start(f32[2,2,64,128]{3,2,1,0:T(8,128)S(1)} %fusion.1), channel_id=1, source_target_pairs={{32,48},{48,64},{64,80},{80,96},{96,112},{112,128},{128,144},{144,... | collective-permute-start | bytes 393224 | tf_op jit(solution)/shard_map/ppermute | solution.py:341
  27.6 1.9 %collective-permute-done.2.rest_2_ = f32[2,2,64,128]{3,2,1,0:T(8,128)S(1)} collective-permute-done((f32[2,2,64,128]{3,2,1,0:T(8,128)S(1)}, f32[2,2,64,128]{3,2,1,0:T(8,128)S(1)}, u32[]{:S(2)}, u32[]{:S(2)}) %collective-permute-start.2) | collective-permute-done | bytes 131104 | tf_op jit(solution)/shard_map/ppermute | solution.py:341
  29.5 0.2 fusion.2
  29.8 5.7 %collective-permute-start.3 = (f32[2,2,64,128]{3,2,1,0:T(8,128)S(1)}, f32[2,2,64,128]{3,2,1,0:T(8,128)S(1)}, u32[]{:S(2)}, u32[]{:S(2)}) collective-permute-start(f32[2,2,64,128]{3,2,1,0:T(8,128)S(1)} %fusion.2), channel_id=1, source_target_pairs={{48,64},{64,80},{80,96},{96,112},{112,128},{128,144},{144,160},{16... | collective-permute-start | bytes 393224 | tf_op jit(solution)/shard_map/ppermute | solution.py:341
  35.5 1.9 %collective-permute-done.3.rest_3_ = f32[2,2,64,128]{3,2,1,0:T(8,128)S(1)} collective-permute-done((f32[2,2,64,128]{3,2,1,0:T(8,128)S(1)}, f32[2,2,64,128]{3,2,1,0:T(8,128)S(1)}, u32[]{:S(2)}, u32[]{:S(2)}) %collective-permute-start.3) | collective-permute-done | bytes 131104 | tf_op jit(solution)/shard_map/ppermute | solution.py:341
  37.5 0.3 shard_map.84
  37.7 20.2 %all-gather = f32[16,256]{1,0:T(8,128)S(1)} all-gather(f32[8,256]{1,0:T(8,128)S(1)} %get-tuple-element.37), channel_id=2, replica_groups=mesh['groups'=2,'seq'=16,'head'=8,'dim'=2] {'dim'}, dimensions={0}, use_global_device_ids=true | all-gather | bytes 24576 | tf_op jit(solution)/shard_map/all_gather | solution.py:349
  58.0 0.8 %shard_map.85 = bf16[2,2,64,256]{3,2,1,0:T(8,128)(2,1)} custom-call(f32[2,2,64,256]{3,2,1,0:T(8,128)S(1)} %get-tuple-element.36.raw, f32[2,8,256]{2,1,0:T(8,128)S(1)} %bitcast.9, bf16[2,2,64,256]{3,2,1,0:T(8,128)(2,1)S(1)} %get-tuple-element.38.gate, f32[1,64]{1,0:T(1,128)S(1)} %get-tuple-element.39.gain, f32[8,256]{1,0:T(8,128)S(1)} %get-tuple-element.40.live), custom_call_target="tpu_custom_call" | custom-call | tf_op jit(solution)/shard_map/pallas_call | solution.py:271
Async XLA Ops:
  4.4 9.1 %collective-permute-start = (f32[2,2,64,128]{3,2,1,0:T(8,128)S(1)}, f32[2,2,64,128]{3,2,1,0:T(8,128)S(1)}, u32[]{:S(2)}, u32[]{:S(2)}) collective-permute-start(f32[2,2,64,128]{3,2,1,0:T(8,128)S(1)} %get-tuple-element.34), channel_id=1, source_target_pairs={{0,16},{16,32},{32,48},{48,64},{64,80},{80,96},{96,112},{112,128},... | collective-permute-start | bytes 393224 | tf_op jit(solution)/shard_map/ppermute | solution.py:321
  13.8 7.7 %collective-permute-start.1 = (f32[2,2,64,128]{3,2,1,0:T(8,128)S(1)}, f32[2,2,64,128]{3,2,1,0:T(8,128)S(1)}, u32[]{:S(2)}, u32[]{:S(2)}) collective-permute-start(f32[2,2,64,128]{3,2,1,0:T(8,128)S(1)} %fusion), channel_id=1, source_target_pairs={{16,32},{32,48},{48,64},{64,80},{80,96},{96,112},{112,128},{128,14... | collective-permute-start | bytes 393224 | tf_op jit(solution)/shard_map/ppermute | solution.py:341
  21.8 7.7 %collective-permute-start.2 = (f32[2,2,64,128]{3,2,1,0:T(8,128)S(1)}, f32[2,2,64,128]{3,2,1,0:T(8,128)S(1)}, u32[]{:S(2)}, u32[]{:S(2)}) collective-permute-start(f32[2,2,64,128]{3,2,1,0:T(8,128)S(1)} %fusion.1), channel_id=1, source_target_pairs={{32,48},{48,64},{64,80},{80,96},{96,112},{112,128},{128,144},{144,... | collective-permute-start | bytes 393224 | tf_op jit(solution)/shard_map/ppermute | solution.py:341
  29.8 7.7 %collective-permute-start.3 = (f32[2,2,64,128]{3,2,1,0:T(8,128)S(1)}, f32[2,2,64,128]{3,2,1,0:T(8,128)S(1)}, u32[]{:S(2)}, u32[]{:S(2)}) collective-permute-start(f32[2,2,64,128]{3,2,1,0:T(8,128)S(1)} %fusion.2), channel_id=1, source_target_pairs={{48,64},{64,80},{80,96},{96,112},{112,128},{128,144},{144,160},{16... | collective-permute-start | bytes 393224 | tf_op jit(solution)/shard_map/ppermute | solution.py:341

commit v3 on v2

--- a/solution.py
+++ b/solution.py
@@ -5,13 +5,25 @@
 from jax.experimental.pallas import tpu as pltpu
 from jax.sharding import PartitionSpec as P
 
-WINDOW = 4
+
 F32 = jnp.float32
 BF16 = jnp.bfloat16
 
 
 def dot(left, right):
     return jnp.dot(left, right, preferred_element_type=F32)
+
+
+def exact_dot(left, right):
+    return jnp.dot(left, right, precision=lax.Precision.HIGH, preferred_element_type=F32)
+
+
+def apply_map(left, right):
+    return jnp.matmul(left, right, precision=lax.Precision.HIGH)
+
+
+def passed(value, distance, first, last):
+    return lax.ppermute(value, "seq", [(s, s + distance) for s in range(first, last)])
 
 
 def split(full):
@@ -59,7 +71,6 @@
     for copy in copies:
         copy.start()
     seqs, heads, tokens, width = key.shape
-    val_width = value.shape[2]
     half = tokens // 2
     pairs = [(b, h) for b in range(seqs) for h in range(heads)]
     count = len(pairs)
@@ -139,11 +150,28 @@
     steps = [high_ref[i, s : s + half, s : s + half] * masks[0] for i, s in blocks]
     twos = [dot(n, n) for n in steps]
     invs = [(low_eye - n.astype(F32) + t - dot(n, t.astype(BF16))).astype(BF16) for n, t in zip(steps, twos)]
+    size = 4
     for mask in masks[1:]:
-        mids = [
-            dot(x, high_ref[i, s : s + half, s : s + half] * mask).astype(BF16) for x, (i, s) in zip(invs, blocks)
-        ]
-        invs = [x - dot(m, x).astype(BF16) for x, m in zip(invs, mids)]
+        links = [high_ref[i, s : s + half, s : s + half] * mask for i, s in blocks]
+        if size < 16:
+            mids = [dot(x, link).astype(BF16) for x, link in zip(invs, links)]
+            invs = [x - dot(m, x).astype(BF16) for x, m in zip(invs, mids)]
+        else:
+            uppers = [jnp.concatenate([x[k : k + size] for k in range(0, half, 2 * size)], axis=0) for x in invs]
+            mids = [dot(u, link).astype(BF16) for u, link in zip(uppers, links)]
+            uppers = [u - dot(m, x).astype(BF16) for u, m, x in zip(uppers, mids, invs)]
+            invs = [
+                jnp.concatenate(
+                    [
+                        piece
+                        for k in range(0, half, 2 * size)
+                        for piece in (u[k // 2 : k // 2 + size], x[k + size : k + 2 * size])
+                    ],
+                    axis=0,
+                )
+                for u, x in zip(uppers, invs)
+            ]
+        size *= 2
     mids = [dot(invs[2 * i], high_ref[i, :half, half:]).astype(BF16) for i in members]
     corners = [-dot(mid, invs[2 * i + 1]).astype(BF16) for i, mid in enumerate(mids)]
     for i in members:
@@ -198,7 +226,9 @@
     )
 
 
-def output_kernel(query, key, value, mix, inv, fix, decay, keys, cum, own_out, carry_out, map_out):
+def output_kernel(
+    query, key, value, mix, inv, fix, decay, keys, cum, gate, gain, live, own_out, carry_out, map_out, factor_out
+):
     seqs, heads, tokens, width = query.shape
     half = tokens // 2
     pairs = [(b, h) for b in range(seqs) for h in range(heads)]
@@ -225,6 +255,10 @@
         whole = jnp.exp(cum[i : i + 1, tokens - 1 :])
         both = from_values_narrow(keys[i, 0], mix[i, 0], mix[i, 1])
         map_out[pair] = whole * eye - (both + dot(keys[i, 1], mix[i, 0]))
+    gains = jnp.broadcast_to(gain[...], (8, gain.shape[1])).T[:, :1]
+    for i, pair in enumerate(pairs):
+        opened = gate[pair].astype(F32)
+        factor_out[pair] = gains * (opened / (1.0 + jnp.exp(-opened))) * live[i : i + 1]
     parts = [split(mixed) for mixed in mixes]
     for i, (high, low) in enumerate(parts):
         own_out[pairs[i]] = from_values(value[pairs[i]], high, low)
@@ -233,35 +267,24 @@
         carry_out[pairs[i]] = queries[i].astype(F32) * jnp.exp(cum[i : i + 1]) - taken
 
 
-def raw_kernel(own, carry, *rest):
-    *states, raw_out, square_out = rest
+def raw_kernel(own, carry, near, next_near, far, product, raw_out, square_out):
     seqs, heads = own.shape[:2]
-    rows = []
-    for b in range(seqs):
-        for h in range(heads):
-            state = states[0][b, h]
-            for arrived in states[1:]:
-                state = state + arrived[b, h]
-            raw = own[b, h] + jnp.dot(
-                state, carry[b, h], precision=lax.Precision.HIGH, preferred_element_type=F32
-            )
-            raw_out[b, h] = raw
-            rows.append(jnp.sum(raw * raw, axis=0, keepdims=True))
-    square_out[...] = stack_rows(rows)
-
-
-def gate_kernel(raw, squares, gate, gain, live, out):
-    seqs, heads, val_width, tokens = raw.shape
+    pairs = [(b, h) for b in range(seqs) for h in range(heads)]
+    states = [(near[pair] + next_near[pair]) + exact_dot(far[pair], product[pair]) for pair in pairs]
+    raws = [own[pair] + exact_dot(state, carry[pair]) for pair, state in zip(pairs, states)]
+    for pair, raw in zip(pairs, raws):
+        raw_out[pair] = raw
+    square_out[...] = stack_rows([jnp.sum(raw * raw, axis=0, keepdims=True) for raw in raws])
+
+
+def gate_kernel(raw, squares, factor, out):
+    seqs, heads, val_width, _ = raw.shape
     total = jnp.sum(squares[...], axis=0)
     scale = lax.rsqrt(total / (val_width * squares.shape[0]) + 1e-06)
-    gains = jnp.broadcast_to(gain[...], (8, val_width)).T[:, :1]
-    scale = scale * live[...]
     for b in range(seqs):
         for h in range(heads):
             i = b * heads + h
-            opened = gate[b, h].astype(F32)
-            opened = opened / (1.0 + jnp.exp(-opened))
-            out[b, h] = (raw[b, h] * scale[i : i + 1] * (gains * opened)).astype(BF16)
+            out[b, h] = (raw[b, h] * scale[i : i + 1] * factor[b, h]).astype(BF16)
 
 
 VMEM = pl.BlockSpec(memory_space=pltpu.VMEM)
@@ -317,14 +340,15 @@
             pltpu.SemaphoreType.DMA((8,)),
         ],
     )
-    steps = lax.axis_size("seq") - 1
-    arrived = [lax.ppermute(block_end, "seq", [(s, s + 1) for s in range(steps)])]
-    own, carry, block_map = call(
+    steps = lax.axis_size("seq")
+    near = passed(block_end, 1, 0, steps - 1)
+    own, carry, block_map, factor = call(
         output_kernel,
         (
             shape((seqs, heads, val_width, tokens), F32),
             shape((seqs, heads, width, tokens), F32),
             shape((seqs, heads, width, width), F32),
+            shape((seqs, heads, val_width, tokens), F32),
         ),
         query,
         key,
@@ -335,16 +359,24 @@
         decay,
         keys,
         cum,
-    )
-    for hop in range(1, WINDOW):
-        moving = jnp.matmul(arrived[-1], block_map, precision=lax.Precision.HIGH)
-        arrived.append(lax.ppermute(moving, "seq", [(s, s + 1) for s in range(hop, steps)]))
+        out_gate,
+        norm_gain,
+        live,
+    )
+    moved = apply_map(near, block_map)
+    far = passed(block_end + moved, 3, 0, steps - 3)
+    next_near = passed(moved, 1, 1, steps - 1)
+    earlier = passed(block_map, 1, 1, steps - 2)
+    product = passed(apply_map(earlier, block_map), 1, 2, steps - 1)
     raw, squares = call(
         raw_kernel,
         (shape((seqs, heads, val_width, tokens), F32), rows),
         own,
         carry,
-        *arrived,
+        near,
+        next_near,
+        far,
+        product,
     )
     squares = lax.all_gather(squares, "dim")
     return call(
@@ -352,9 +384,7 @@
         shape((seqs, heads, val_width, tokens), BF16),
         raw,
         squares,
-        out_gate,
-        norm_gain,
-        live,
+        factor,
     )
 
 

time: 59 us -> 58.9 us (level)
  the two profiles are of different devices: /device:TPU:833 before, /device:TPU:65 now
where the time goes in v3:
time: 58.9 us; the launch traced here: 58.7 us
  starting transfers between devices  31.8 us (54%)
  blocking collectives  16.9 us (29%)
  Pallas kernels  7.09 us (12%)
  waiting for transfers between devices  2.2 us (4%)
    ppermute x5, starting transfers between devices, passed(): lax.ppermute(value, 'seq', [(s, s + distance) for s in range(first, last)])  31.8 us
    all_gather x1, blocking collectives, local(): squares = lax.all_gather(squares, 'dim')  16.9 us
    pallas_call x4, Pallas kernels, call(): pl.pallas_call(body, out_shape=outs, in_specs=[space] * len(operands), ou...  7.09 us
    ppermute x5, waiting for transfers between devices, passed(): lax.ppermute(value, 'seq', [(s, s + distance) for s in range(first, last)])  2.2 us
  transfers between devices with their start and end apart: 5, of which 2 were waited for; matrix products, arithmetic and copies ran while one was open for 1% of the time, Pallas kernels for 0%

profile of v3, /device:TPU:65, one launch (start us, length us, event | category | flops | bytes accessed | tf_op | source)
XLA Modules:
  0.0 58.7 jit_solution(2006185071144429004)
XLA Ops:
  0.0 4.4 %shard_map.82 = (f32[2,2,64,128]{3,2,1,0:T(8,128)S(1)}, bf16[4,2,256,128]{3,2,1,0:T(8,128)(2,1)S(1)}, bf16[4,256,256]{2,1,0:T(8,128)(2,1)S(1)}, bf16[4,256,256]{...) custom-call(s32[1,2]{1,0:T(1,128)} %bitcast.8, ...), custom_call_target="tpu_custom_call" | custom-call | tf_op jit(solution)/shard_map/pallas_call | solution.py:294
  4.4 1.5 %shard_map.83 = (f32[2,2,64,256]{3,2,1,0:T(8,128)S(1)}, f32[2,2,128,256]{3,2,1,0:T(8,128)S(1)}, f32[2,2,128,128]{3,2,1,0:T(8,128)S(1)}, f32[2,2,64,256]{3,2,1,0:T(8,128)S(1)}) custom-call(bf16[2,2,256,128]{3,2,1,0:T(8,128)(2,1)S(1)} %get-tuple-element.24.query, bf16[2,2,256,128]{3,2,1,0:T(8,128)(2,1)S(1)} %get-tuple-element.25.key, ...), custom_call_target="tpu_custom_call" | custom-call | tf_op jit(solution)/shard_map/pallas_call | solution.py:294
  6.0 0.7 %collective-permute-start.3 = (f32[2,2,128,128]{3,2,1,0:T(8,128)S(1)}, f32[2,2,128,128]{3,2,1,0:T(8,128)S(1)}, u32[]{:S(2)}, u32[]{:S(2)}) collective-permute-start(f32[2,2,128,128]{3,2,1,0:T(8,128)S(1)} %get-tuple-element.39), channel_id=1, source_target_pairs={{16,32},{32,48},{48,64},{64,80},{80,96},{96,112},{112,128},{128,14... | collective-permute-start | bytes 786440 | tf_op jit(solution)/shard_map/ppermute | solution.py:26
  6.7 11.7 %collective-permute-start = (f32[2,2,64,128]{3,2,1,0:T(8,128)S(1)}, f32[2,2,64,128]{3,2,1,0:T(8,128)S(1)}, u32[]{:S(2)}, u32[]{:S(2)}) collective-permute-start(f32[2,2,64,128]{3,2,1,0:T(8,128)S(1)} %get-tuple-element.38), channel_id=1, source_target_pairs={{0,16},{16,32},{32,48},{48,64},{64,80},{80,96},{96,112},{112,128},... | collective-permute-start | bytes 393224 | tf_op jit(solution)/shard_map/ppermute | solution.py:26
  18.3 0.0 collective-permute-done.3
  18.3 0.3 fusion.1
  18.6 0.7 %collective-permute-start.4 = (f32[2,2,128,128]{3,2,1,0:T(8,128)S(1)}, f32[2,2,128,128]{3,2,1,0:T(8,128)S(1)}, u32[]{:S(2)}, u32[]{:S(2)}) collective-permute-start(f32[2,2,128,128]{3,2,1,0:T(8,128)S(1)} %fusion.1), channel_id=1, source_target_pairs={{32,48},{48,64},{64,80},{80,96},{96,112},{112,128},{128,144},{144,... | collective-permute-start | bytes 786440 | tf_op jit(solution)/shard_map/ppermute | solution.py:26
  19.3 0.9 %collective-permute-done.near = f32[2,2,64,128]{3,2,1,0:T(8,128)S(1)} collective-permute-done((f32[2,2,64,128]{3,2,1,0:T(8,128)S(1)}, f32[2,2,64,128]{3,2,1,0:T(8,128)S(1)}, u32[]{:S(2)}, u32[]{:S(2)}) %collective-permute-start) | collective-permute-done | bytes 131104 | tf_op jit(solution)/shard_map/ppermute | solution.py:26
  20.3 0.2 fusion
  20.5 18.1 %collective-permute-start.2 = (f32[2,2,64,128]{3,2,1,0:T(8,128)S(1)}, f32[2,2,64,128]{3,2,1,0:T(8,128)S(1)}, u32[]{:S(2)}, u32[]{:S(2)}) collective-permute-start(f32[2,2,64,128]{3,2,1,0:T(8,128)S(1)} %get-tuple-element.43), channel_id=1, source_target_pairs={{0,48},{16,64},{32,80},{48,96},{64,112},{80,128},{96,144},{112,160... | collective-permute-start | bytes 393224 | tf_op jit(solution)/shard_map/ppermute | solution.py:26
  38.6 0.7 %collective-permute-start.1 = (f32[2,2,64,128]{3,2,1,0:T(8,128)S(1)}, f32[2,2,64,128]{3,2,1,0:T(8,128)S(1)}, u32[]{:S(2)}, u32[]{:S(2)}) collective-permute-start(f32[2,2,64,128]{3,2,1,0:T(8,128)S(1)} %get-tuple-element.44), channel_id=1, source_target_pairs={{16,32},{32,48},{48,64},{64,80},{80,96},{96,112},{112,128},{128,14... | collective-permute-start | bytes 393224 | tf_op jit(solution)/shard_map/ppermute | solution.py:26
  39.3 1.2 %collective-permute-done.2.far = f32[2,2,64,128]{3,2,1,0:T(8,128)S(1)} collective-permute-done((f32[2,2,64,128]{3,2,1,0:T(8,128)S(1)}, f32[2,2,64,128]{3,2,1,0:T(8,128)S(1)}, u32[]{:S(2)}, u32[]{:S(2)}) %collective-permute-start.2) | collective-permute-done | bytes 131104 | tf_op jit(solution)/shard_map/ppermute | solution.py:26
  40.6 0.0 collective-permute-done.1.next_near
  40.6 0.0 collective-permute-done.4.product
  40.6 0.4 shard_map.84
  41.0 16.9 %all-gather = f32[16,256]{1,0:T(8,128)S(1)} all-gather(f32[8,256]{1,0:T(8,128)S(1)} %get-tuple-element.41), channel_id=2, replica_groups=mesh['groups'=2,'seq'=16,'head'=8,'dim'=2] {'dim'}, dimensions={0}, use_global_device_ids=true | all-gather | bytes 24576 | tf_op jit(solution)/shard_map/all_gather | solution.py:381
  58.0 0.7 %shard_map.85 = bf16[2,2,64,256]{3,2,1,0:T(8,128)(2,1)} custom-call(f32[2,2,64,256]{3,2,1,0:T(8,128)S(1)} %get-tuple-element.40.raw, f32[2,8,256]{2,1,0:T(8,128)S(1)} %bitcast.7, f32[2,2,64,256]{3,2,1,0:T(8,128)S(1)} %get-tuple-element.42.factor), custom_call_target="tpu_custom_call" | custom-call | tf_op jit(solution)/shard_map/pallas_call | solution.py:294
Async XLA Ops:
  6.0 12.3 %collective-permute-start.3 = (f32[2,2,128,128]{3,2,1,0:T(8,128)S(1)}, f32[2,2,128,128]{3,2,1,0:T(8,128)S(1)}, u32[]{:S(2)}, u32[]{:S(2)}) collective-permute-start(f32[2,2,128,128]{3,2,1,0:T(8,128)S(1)} %get-tuple-element.39), channel_id=1, source_target_pairs={{16,32},{32,48},{48,64},{64,80},{80,96},{96,112},{112,128},{128,14... | collective-permute-start | bytes 786440 | tf_op jit(solution)/shard_map/ppermute | solution.py:26
  6.7 13.6 %collective-permute-start = (f32[2,2,64,128]{3,2,1,0:T(8,128)S(1)}, f32[2,2,64,128]{3,2,1,0:T(8,128)S(1)}, u32[]{:S(2)}, u32[]{:S(2)}) collective-permute-start(f32[2,2,64,128]{3,2,1,0:T(8,128)S(1)} %get-tuple-element.38), channel_id=1, source_target_pairs={{0,16},{16,32},{32,48},{48,64},{64,80},{80,96},{96,112},{112,128},... | collective-permute-start | bytes 393224 | tf_op jit(solution)/shard_map/ppermute | solution.py:26
  18.6 21.9 %collective-permute-start.4 = (f32[2,2,128,128]{3,2,1,0:T(8,128)S(1)}, f32[2,2,128,128]{3,2,1,0:T(8,128)S(1)}, u32[]{:S(2)}, u32[]{:S(2)}) collective-permute-start(f32[2,2,128,128]{3,2,1,0:T(8,128)S(1)} %fusion.1), channel_id=1, source_target_pairs={{32,48},{48,64},{64,80},{80,96},{96,112},{112,128},{128,144},{144,... | collective-permute-start | bytes 786440 | tf_op jit(solution)/shard_map/ppermute | solution.py:26
  20.5 20.1 %collective-permute-start.2 = (f32[2,2,64,128]{3,2,1,0:T(8,128)S(1)}, f32[2,2,64,128]{3,2,1,0:T(8,128)S(1)}, u32[]{:S(2)}, u32[]{:S(2)}) collective-permute-start(f32[2,2,64,128]{3,2,1,0:T(8,128)S(1)} %get-tuple-element.43), channel_id=1, source_target_pairs={{0,48},{16,64},{32,80},{48,96},{64,112},{80,128},{96,144},{112,160... | collective-permute-start | bytes 393224 | tf_op jit(solution)/shard_map/ppermute | solution.py:26
  38.6 1.9 %collective-permute-start.1 = (f32[2,2,64,128]{3,2,1,0:T(8,128)S(1)}, f32[2,2,64,128]{3,2,1,0:T(8,128)S(1)}, u32[]{:S(2)}, u32[]{:S(2)}) collective-permute-start(f32[2,2,64,128]{3,2,1,0:T(8,128)S(1)} %get-tuple-element.44), channel_id=1, source_target_pairs={{16,32},{32,48},{48,64},{64,80},{80,96},{96,112},{112,128},{128,14... | collective-permute-start | bytes 393224 | tf_op jit(solution)/shard_map/ppermute | solution.py:26

commit v4 on v3

--- a/solution.py
+++ b/solution.py
@@ -143,8 +143,7 @@
         high_ref[i, half:, :half] = jnp.zeros((half, half), BF16)
         low_ref[i, half:, :half] = jnp.zeros((half, half), BF16)
 
-    for copy in copies[4:]:
-        copy.wait()
+    copies[4].wait()
     members = range(count)
     blocks = [(i, s) for i in members for s in (0, half)]
     steps = [high_ref[i, s : s + half, s : s + half] * masks[0] for i, s in blocks]
@@ -209,6 +208,8 @@
         key_high, key_low = split(keys_t[i].astype(F32) * (jnp.exp(cums[i]) * norms[i]))
         keys_out[i, 0] = key_high
         keys_out[i, 1] = key_low
+    for copy in copies[5:]:
+        copy.wait()
 
 
 def from_values(value, high, low):
@@ -267,10 +268,10 @@
         carry_out[pairs[i]] = queries[i].astype(F32) * jnp.exp(cum[i : i + 1]) - taken
 
 
-def raw_kernel(own, carry, near, next_near, far, product, raw_out, square_out):
+def raw_kernel(own, carry, near, next_near, first, far, product, raw_out, square_out):
     seqs, heads = own.shape[:2]
     pairs = [(b, h) for b in range(seqs) for h in range(heads)]
-    states = [(near[pair] + next_near[pair]) + exact_dot(far[pair], product[pair]) for pair in pairs]
+    states = [(near[pair] + next_near[pair]) + exact_dot(first[pair] + far[pair], product[pair]) for pair in pairs]
     raws = [own[pair] + exact_dot(state, carry[pair]) for pair, state in zip(pairs, states)]
     for pair, raw in zip(pairs, raws):
         raw_out[pair] = raw
@@ -342,6 +343,7 @@
     )
     steps = lax.axis_size("seq")
     near = passed(block_end, 1, 0, steps - 1)
+    first = passed(block_end, 3, 0, 1)
     own, carry, block_map, factor = call(
         output_kernel,
         (
@@ -364,7 +366,7 @@
         live,
     )
     moved = apply_map(near, block_map)
-    far = passed(block_end + moved, 3, 0, steps - 3)
+    far = passed(block_end + moved, 3, 1, steps - 3)
     next_near = passed(moved, 1, 1, steps - 1)
     earlier = passed(block_map, 1, 1, steps - 2)
     product = passed(apply_map(earlier, block_map), 1, 2, steps - 1)
@@ -375,6 +377,7 @@
         carry,
         near,
         next_near,
+        first,
         far,
         product,
     )

time: 58.9 us -> 59.2 us (level)
  the two profiles are of different devices: /device:TPU:65 before, /device:TPU:321 now
where the time goes in v4:
time: 59.2 us; the launch traced here: 59 us
  starting transfers between devices  30.9 us (52%)
  waiting for transfers between devices  11.3 us (19%)
  blocking collectives  9.08 us (15%)
  Pallas kernels  7.09 us (12%)
    ppermute x6, starting transfers between devices, passed(): lax.ppermute(value, 'seq', [(s, s + distance) for s in range(first, last)])  30.9 us
    ppermute x6, waiting for transfers between devices, passed(): lax.ppermute(value, 'seq', [(s, s + distance) for s in range(first, last)])  11.3 us
    all_gather x1, blocking collectives, local(): squares = lax.all_gather(squares, 'dim')  9.08 us
    pallas_call x4, Pallas kernels, call(): pl.pallas_call(body, out_shape=outs, in_specs=[space] * len(operands), ou...  7.09 us
  transfers between devices with their start and end apart: 6, of which 2 were waited for; matrix products, arithmetic and copies ran while one was open for 1% of the time, Pallas kernels for 0%

profile of v4, /device:TPU:321, one launch (start us, length us, event | category | flops | bytes accessed | tf_op | source)
XLA Modules:
  0.0 59.0 jit_solution(8374276217372955355)
XLA Ops:
  0.0 4.4 %shard_map.82 = (f32[2,2,64,128]{3,2,1,0:T(8,128)S(1)}, bf16[4,2,256,128]{3,2,1,0:T(8,128)(2,1)S(1)}, bf16[4,256,256]{2,1,0:T(8,128)(2,1)S(1)}, bf16[4,256,256]{...) custom-call(s32[1,2]{1,0:T(1,128)} %bitcast.8, ...), custom_call_target="tpu_custom_call" | custom-call | tf_op jit(solution)/shard_map/pallas_call | solution.py:295
  4.4 1.5 %shard_map.83 = (f32[2,2,64,256]{3,2,1,0:T(8,128)S(1)}, f32[2,2,128,256]{3,2,1,0:T(8,128)S(1)}, f32[2,2,128,128]{3,2,1,0:T(8,128)S(1)}, f32[2,2,64,256]{3,2,1,0:T(8,128)S(1)}) custom-call(bf16[2,2,256,128]{3,2,1,0:T(8,128)(2,1)S(1)} %get-tuple-element.24.query, bf16[2,2,256,128]{3,2,1,0:T(8,128)(2,1)S(1)} %get-tuple-element.25.key, ...), custom_call_target="tpu_custom_call" | custom-call | tf_op jit(solution)/shard_map/pallas_call | solution.py:295
  6.0 5.8 %collective-permute-start.4 = (f32[2,2,128,128]{3,2,1,0:T(8,128)S(1)}, f32[2,2,128,128]{3,2,1,0:T(8,128)S(1)}, u32[]{:S(2)}, u32[]{:S(2)}) collective-permute-start(f32[2,2,128,128]{3,2,1,0:T(8,128)S(1)} %get-tuple-element.39), channel_id=1, source_target_pairs={{16,32},{32,48},{48,64},{64,80},{80,96},{96,112},{112,128},{128,14... | collective-permute-start | bytes 786440 | tf_op jit(solution)/shard_map/ppermute | solution.py:26
  11.7 0.7 %collective-permute-start.2 = (f32[2,2,64,128]{3,2,1,0:T(8,128)S(1)}, f32[2,2,64,128]{3,2,1,0:T(8,128)S(1)}, u32[]{:S(2)}, u32[]{:S(2)}) collective-permute-start(f32[2,2,64,128]{3,2,1,0:T(8,128)S(1)} %get-tuple-element.38), channel_id=1, source_target_pairs={{0,48},{1,49},{2,50},{3,51},{4,52},{5,53},{6,54},{7,55},{8,56},{9,... | collective-permute-start | bytes 393224 | tf_op jit(solution)/shard_map/ppermute | solution.py:26
  12.4 5.7 %collective-permute-start = (f32[2,2,64,128]{3,2,1,0:T(8,128)S(1)}, f32[2,2,64,128]{3,2,1,0:T(8,128)S(1)}, u32[]{:S(2)}, u32[]{:S(2)}) collective-permute-start(f32[2,2,64,128]{3,2,1,0:T(8,128)S(1)} %get-tuple-element.38), channel_id=1, source_target_pairs={{0,16},{16,32},{32,48},{48,64},{64,80},{80,96},{96,112},{112,128},... | collective-permute-start | bytes 393224 | tf_op jit(solution)/shard_map/ppermute | solution.py:26
  18.2 0.0 collective-permute-done.4
  18.2 0.3 fusion.1
  18.5 0.7 %collective-permute-start.5 = (f32[2,2,128,128]{3,2,1,0:T(8,128)S(1)}, f32[2,2,128,128]{3,2,1,0:T(8,128)S(1)}, u32[]{:S(2)}, u32[]{:S(2)}) collective-permute-start(f32[2,2,128,128]{3,2,1,0:T(8,128)S(1)} %fusion.1), channel_id=1, source_target_pairs={{32,48},{48,64},{64,80},{80,96},{96,112},{112,128},{128,144},{144,... | collective-permute-start | bytes 786440 | tf_op jit(solution)/shard_map/ppermute | solution.py:26
  19.1 8.0 %collective-permute-done.near = f32[2,2,64,128]{3,2,1,0:T(8,128)S(1)} collective-permute-done((f32[2,2,64,128]{3,2,1,0:T(8,128)S(1)}, f32[2,2,64,128]{3,2,1,0:T(8,128)S(1)}, u32[]{:S(2)}, u32[]{:S(2)}) %collective-permute-start) | collective-permute-done | bytes 131104 | tf_op jit(solution)/shard_map/ppermute | solution.py:26
  27.1 0.2 fusion
  27.4 11.1 %collective-permute-start.3 = (f32[2,2,64,128]{3,2,1,0:T(8,128)S(1)}, f32[2,2,64,128]{3,2,1,0:T(8,128)S(1)}, u32[]{:S(2)}, u32[]{:S(2)}) collective-permute-start(f32[2,2,64,128]{3,2,1,0:T(8,128)S(1)} %get-tuple-element.43), channel_id=1, source_target_pairs={{16,64},{32,80},{48,96},{64,112},{80,128},{96,144},{112,160},{128,... | collective-permute-start | bytes 393224 | tf_op jit(solution)/shard_map/ppermute | solution.py:26
  38.5 7.0 %collective-permute-start.1 = (f32[2,2,64,128]{3,2,1,0:T(8,128)S(1)}, f32[2,2,64,128]{3,2,1,0:T(8,128)S(1)}, u32[]{:S(2)}, u32[]{:S(2)}) collective-permute-start(f32[2,2,64,128]{3,2,1,0:T(8,128)S(1)} %get-tuple-element.44), channel_id=1, source_target_pairs={{16,32},{32,48},{48,64},{64,80},{80,96},{96,112},{112,128},{128,14... | collective-permute-start | bytes 393224 | tf_op jit(solution)/shard_map/ppermute | solution.py:26
  45.5 0.0 collective-permute-done.2.first
  45.5 0.0 collective-permute-done.3.far
  45.5 3.3 %collective-permute-done.1.next_near = f32[2,2,64,128]{3,2,1,0:T(8,128)S(1)} collective-permute-done((f32[2,2,64,128]{3,2,1,0:T(8,128)S(1)}, f32[2,2,64,128]{3,2,1,0:T(8,128)S(1)}, u32[]{:S(2)}, u32[]{:S(2)}) %collective-permute-start.1) | collective-permute-done | bytes 131104 | tf_op jit(solution)/shard_map/ppermute | solution.py:26
  48.8 0.0 collective-permute-done.5.product
  48.8 0.4 shard_map.84
  49.2 9.1 %all-gather = f32[16,256]{1,0:T(8,128)S(1)} all-gather(f32[8,256]{1,0:T(8,128)S(1)} %get-tuple-element.41), channel_id=2, replica_groups=mesh['groups'=2,'seq'=16,'head'=8,'dim'=2] {'dim'}, dimensions={0}, use_global_device_ids=true | all-gather | bytes 24576 | tf_op jit(solution)/shard_map/all_gather | solution.py:384
  58.3 0.7 %shard_map.85 = bf16[2,2,64,256]{3,2,1,0:T(8,128)(2,1)} custom-call(f32[2,2,64,256]{3,2,1,0:T(8,128)S(1)} %get-tuple-element.40.raw, f32[2,8,256]{2,1,0:T(8,128)S(1)} %bitcast.7, f32[2,2,64,256]{3,2,1,0:T(8,128)S(1)} %get-tuple-element.42.factor), custom_call_target="tpu_custom_call" | custom-call | tf_op jit(solution)/shard_map/pallas_call | solution.py:295
Async XLA Ops:
  6.0 12.2 %collective-permute-start.4 = (f32[2,2,128,128]{3,2,1,0:T(8,128)S(1)}, f32[2,2,128,128]{3,2,1,0:T(8,128)S(1)}, u32[]{:S(2)}, u32[]{:S(2)}) collective-permute-start(f32[2,2,128,128]{3,2,1,0:T(8,128)S(1)} %get-tuple-element.39), channel_id=1, source_target_pairs={{16,32},{32,48},{48,64},{64,80},{80,96},{96,112},{112,128},{128,14... | collective-permute-start | bytes 786440 | tf_op jit(solution)/shard_map/ppermute | solution.py:26
  11.7 33.7 %collective-permute-start.2 = (f32[2,2,64,128]{3,2,1,0:T(8,128)S(1)}, f32[2,2,64,128]{3,2,1,0:T(8,128)S(1)}, u32[]{:S(2)}, u32[]{:S(2)}) collective-permute-start(f32[2,2,64,128]{3,2,1,0:T(8,128)S(1)} %get-tuple-element.38), channel_id=1, source_target_pairs={{0,48},{1,49},{2,50},{3,51},{4,52},{5,53},{6,54},{7,55},{8,56},{9,... | collective-permute-start | bytes 393224 | tf_op jit(solution)/shard_map/ppermute | solution.py:26
  12.4 14.7 %collective-permute-start = (f32[2,2,64,128]{3,2,1,0:T(8,128)S(1)}, f32[2,2,64,128]{3,2,1,0:T(8,128)S(1)}, u32[]{:S(2)}, u32[]{:S(2)}) collective-permute-start(f32[2,2,64,128]{3,2,1,0:T(8,128)S(1)} %get-tuple-element.38), channel_id=1, source_target_pairs={{0,16},{16,32},{32,48},{48,64},{64,80},{80,96},{96,112},{112,128},... | collective-permute-start | bytes 393224 | tf_op jit(solution)/shard_map/ppermute | solution.py:26
  18.5 30.3 %collective-permute-start.5 = (f32[2,2,128,128]{3,2,1,0:T(8,128)S(1)}, f32[2,2,128,128]{3,2,1,0:T(8,128)S(1)}, u32[]{:S(2)}, u32[]{:S(2)}) collective-permute-start(f32[2,2,128,128]{3,2,1,0:T(8,128)S(1)} %fusion.1), channel_id=1, source_target_pairs={{32,48},{48,64},{64,80},{80,96},{96,112},{112,128},{128,144},{144,... | collective-permute-start | bytes 786440 | tf_op jit(solution)/shard_map/ppermute | solution.py:26
  27.4 18.1 %collective-permute-start.3 = (f32[2,2,64,128]{3,2,1,0:T(8,128)S(1)}, f32[2,2,64,128]{3,2,1,0:T(8,128)S(1)}, u32[]{:S(2)}, u32[]{:S(2)}) collective-permute-start(f32[2,2,64,128]{3,2,1,0:T(8,128)S(1)} %get-tuple-element.43), channel_id=1, source_target_pairs={{16,64},{32,80},{48,96},{64,112},{80,128},{96,144},{112,160},{128,... | collective-permute-start | bytes 393224 | tf_op jit(solution)/shard_map/ppermute | solution.py:26
  38.5 10.3 %collective-permute-start.1 = (f32[2,2,64,128]{3,2,1,0:T(8,128)S(1)}, f32[2,2,64,128]{3,2,1,0:T(8,128)S(1)}, u32[]{:S(2)}, u32[]{:S(2)}) collective-permute-start(f32[2,2,64,128]{3,2,1,0:T(8,128)S(1)} %get-tuple-element.44), channel_id=1, source_target_pairs={{16,32},{32,48},{48,64},{64,80},{80,96},{96,112},{112,128},{128,14... | collective-permute-start | bytes 393224 | tf_op jit(solution)/shard_map/ppermute | solution.py:26

commit v5 on v4

--- a/solution.py
+++ b/solution.py
@@ -89,6 +89,9 @@
         masks.append(((apart >= size) & (apart < 2 * size)).astype(BF16))
         size *= 2
 
+    for ref in (high_ref, low_ref, inv_out, fix_out):
+        for i in range(count):
+            ref[i, half:, :half] = jnp.zeros((half, half), BF16)
     for copy in copies[:2]:
         copy.wait()
     live = [lane < lengths[0, b] for b, _ in pairs]
@@ -140,9 +143,6 @@
             high, low = split(link)
             high_ref[i, r : r + half, c : c + half] = high
             low_ref[i, r : r + half, c : c + half] = low
-        high_ref[i, half:, :half] = jnp.zeros((half, half), BF16)
-        low_ref[i, half:, :half] = jnp.zeros((half, half), BF16)
-
     copies[4].wait()
     members = range(count)
     blocks = [(i, s) for i in members for s in (0, half)]
@@ -176,7 +176,6 @@
     for i in members:
         inv_out[i, :half, :half] = invs[2 * i]
         inv_out[i, :half, half:] = corners[i]
-        inv_out[i, half:, :half] = jnp.zeros_like(corners[i])
         inv_out[i, half:, half:] = invs[2 * i + 1]
     sides = [split(key[pairs[i]].astype(F32) * columns[:, count + i : count + i + 1]) for i in members]
     tops = [
@@ -196,7 +195,6 @@
     mixes = [dot(inv_out[i], jnp.concatenate(sides[i], axis=1)) for i in members]
     for i in members:
         fix_out[i, :half] = (wide_eye - inv_out[i, :half].astype(F32) - tops[i]).astype(BF16)
-        fix_out[i, half:, :half] = jnp.zeros((half, half), BF16)
         fix_out[i, half:, half:] = (low_eye - invs[2 * i + 1].astype(F32) - bottoms[i]).astype(BF16)
     mixes = [mixed[:, :width] + mixed[:, width:] for mixed in mixes]
     parts = [split(mixed + dot(fix_out[i], mixed.astype(BF16))) for i, mixed in enumerate(mixes)]
@@ -242,12 +240,24 @@
         bottom = bottom * decay[i, half:, half:]
         bottom = jnp.concatenate([jnp.zeros_like(bottom), bottom], axis=1)
         parts.append(split(jnp.concatenate([top * decay[i, :half], bottom], axis=0)))
-    mixes = [
+    fixes = [fixed.astype(BF16) for fixed in fixes]
+    wides = [
         dot(
-            jnp.concatenate([inv[i], inv[i], fixes[i].astype(BF16)], axis=1),
+            jnp.concatenate([inv[i, :half], inv[i, :half], fixes[i][:half]], axis=1),
             jnp.concatenate([high, low, high], axis=0),
         )
         for i, (high, low) in enumerate(parts)
+    ]
+    corners = [
+        dot(
+            jnp.concatenate([inv[i, half:, half:], inv[i, half:, half:], fixes[i][half:, half:]], axis=1),
+            jnp.concatenate([high[half:, half:], low[half:, half:], high[half:, half:]], axis=0),
+        )
+        for i, (high, low) in enumerate(parts)
+    ]
+    mixes = [
+        jnp.concatenate([wide, jnp.concatenate([jnp.zeros_like(corner), corner], axis=1)], axis=0)
+        for wide, corner in zip(wides, corners)
     ]
     eye = (
         lax.broadcasted_iota(jnp.int32, (width, width), 0) == lax.broadcasted_iota(jnp.int32, (width, width), 1)

time: 59.2 us -> 59.1 us (level)
  no operation moved by 1% of the time
where the time goes in v5:
time: 59.1 us; the launch traced here: 58.8 us
  starting transfers between devices  30.9 us (52%)
  waiting for transfers between devices  11.3 us (19%)
  blocking collectives  9.08 us (15%)
  Pallas kernels  6.92 us (12%)
    ppermute x6, starting transfers between devices, passed(): lax.ppermute(value, 'seq', [(s, s + distance) for s in range(first, last)])  30.9 us
    ppermute x6, waiting for transfers between devices, passed(): lax.ppermute(value, 'seq', [(s, s + distance) for s in range(first, last)])  11.3 us
    all_gather x1, blocking collectives, local(): squares = lax.all_gather(squares, 'dim')  9.08 us
    pallas_call x4, Pallas kernels, call(): pl.pallas_call(body, out_shape=outs, in_specs=[space] * len(operands), ou...  6.92 us
  transfers between devices with their start and end apart: 6, of which 2 were waited for; matrix products, arithmetic and copies ran while one was open for 1% of the time, Pallas kernels for 0%

profile of v5, /device:TPU:321, one launch (start us, length us, event | category | flops | bytes accessed | tf_op | source)
XLA Modules:
  0.0 58.8 jit_solution(15030294453382291176)
XLA Ops:
  0.0 4.4 %shard_map.82 = (f32[2,2,64,128]{3,2,1,0:T(8,128)S(1)}, bf16[4,2,256,128]{3,2,1,0:T(8,128)(2,1)S(1)}, bf16[4,256,256]{2,1,0:T(8,128)(2,1)S(1)}, bf16[4,256,256]{...) custom-call(s32[1,2]{1,0:T(1,128)} %bitcast.8, ...), custom_call_target="tpu_custom_call" | custom-call | tf_op jit(solution)/shard_map/pallas_call | solution.py:305
  4.4 1.4 %shard_map.83 = (f32[2,2,64,256]{3,2,1,0:T(8,128)S(1)}, f32[2,2,128,256]{3,2,1,0:T(8,128)S(1)}, f32[2,2,128,128]{3,2,1,0:T(8,128)S(1)}, f32[2,2,64,256]{3,2,1,0:T(8,128)S(1)}) custom-call(bf16[2,2,256,128]{3,2,1,0:T(8,128)(2,1)S(1)} %get-tuple-element.24.query, bf16[2,2,256,128]{3,2,1,0:T(8,128)(2,1)S(1)} %get-tuple-element.25.key, ...), custom_call_target="tpu_custom_call" | custom-call | tf_op jit(solution)/shard_map/pallas_call | solution.py:305
  5.8 5.8 %collective-permute-start.4 = (f32[2,2,128,128]{3,2,1,0:T(8,128)S(1)}, f32[2,2,128,128]{3,2,1,0:T(8,128)S(1)}, u32[]{:S(2)}, u32[]{:S(2)}) collective-permute-start(f32[2,2,128,128]{3,2,1,0:T(8,128)S(1)} %get-tuple-element.39), channel_id=1, source_target_pairs={{16,32},{32,48},{48,64},{64,80},{80,96},{96,112},{112,128},{128,14... | collective-permute-start | bytes 786440 | tf_op jit(solution)/shard_map/ppermute | solution.py:26
  11.6 0.7 %collective-permute-start.2 = (f32[2,2,64,128]{3,2,1,0:T(8,128)S(1)}, f32[2,2,64,128]{3,2,1,0:T(8,128)S(1)}, u32[]{:S(2)}, u32[]{:S(2)}) collective-permute-start(f32[2,2,64,128]{3,2,1,0:T(8,128)S(1)} %get-tuple-element.38), channel_id=1, source_target_pairs={{0,48},{1,49},{2,50},{3,51},{4,52},{5,53},{6,54},{7,55},{8,56},{9,... | collective-permute-start | bytes 393224 | tf_op jit(solution)/shard_map/ppermute | solution.py:26
  12.2 5.7 %collective-permute-start = (f32[2,2,64,128]{3,2,1,0:T(8,128)S(1)}, f32[2,2,64,128]{3,2,1,0:T(8,128)S(1)}, u32[]{:S(2)}, u32[]{:S(2)}) collective-permute-start(f32[2,2,64,128]{3,2,1,0:T(8,128)S(1)} %get-tuple-element.38), channel_id=1, source_target_pairs={{0,16},{16,32},{32,48},{48,64},{64,80},{80,96},{96,112},{112,128},... | collective-permute-start | bytes 393224 | tf_op jit(solution)/shard_map/ppermute | solution.py:26
  18.0 0.0 collective-permute-done.4
  18.0 0.3 fusion.1
  18.3 0.7 %collective-permute-start.5 = (f32[2,2,128,128]{3,2,1,0:T(8,128)S(1)}, f32[2,2,128,128]{3,2,1,0:T(8,128)S(1)}, u32[]{:S(2)}, u32[]{:S(2)}) collective-permute-start(f32[2,2,128,128]{3,2,1,0:T(8,128)S(1)} %fusion.1), channel_id=1, source_target_pairs={{32,48},{48,64},{64,80},{80,96},{96,112},{112,128},{128,144},{144,... | collective-permute-start | bytes 786440 | tf_op jit(solution)/shard_map/ppermute | solution.py:26
  19.0 8.0 %collective-permute-done.near = f32[2,2,64,128]{3,2,1,0:T(8,128)S(1)} collective-permute-done((f32[2,2,64,128]{3,2,1,0:T(8,128)S(1)}, f32[2,2,64,128]{3,2,1,0:T(8,128)S(1)}, u32[]{:S(2)}, u32[]{:S(2)}) %collective-permute-start) | collective-permute-done | bytes 131104 | tf_op jit(solution)/shard_map/ppermute | solution.py:26
  27.0 0.2 fusion
  27.2 11.1 %collective-permute-start.3 = (f32[2,2,64,128]{3,2,1,0:T(8,128)S(1)}, f32[2,2,64,128]{3,2,1,0:T(8,128)S(1)}, u32[]{:S(2)}, u32[]{:S(2)}) collective-permute-start(f32[2,2,64,128]{3,2,1,0:T(8,128)S(1)} %get-tuple-element.43), channel_id=1, source_target_pairs={{16,64},{32,80},{48,96},{64,112},{80,128},{96,144},{112,160},{128,... | collective-permute-start | bytes 393224 | tf_op jit(solution)/shard_map/ppermute | solution.py:26
  38.3 7.0 %collective-permute-start.1 = (f32[2,2,64,128]{3,2,1,0:T(8,128)S(1)}, f32[2,2,64,128]{3,2,1,0:T(8,128)S(1)}, u32[]{:S(2)}, u32[]{:S(2)}) collective-permute-start(f32[2,2,64,128]{3,2,1,0:T(8,128)S(1)} %get-tuple-element.44), channel_id=1, source_target_pairs={{16,32},{32,48},{48,64},{64,80},{80,96},{96,112},{112,128},{128,14... | collective-permute-start | bytes 393224 | tf_op jit(solution)/shard_map/ppermute | solution.py:26
  45.3 0.0 collective-permute-done.2.first
  45.3 0.0 collective-permute-done.3.far
  45.3 3.3 %collective-permute-done.1.next_near = f32[2,2,64,128]{3,2,1,0:T(8,128)S(1)} collective-permute-done((f32[2,2,64,128]{3,2,1,0:T(8,128)S(1)}, f32[2,2,64,128]{3,2,1,0:T(8,128)S(1)}, u32[]{:S(2)}, u32[]{:S(2)}) %collective-permute-start.1) | collective-permute-done | bytes 131104 | tf_op jit(solution)/shard_map/ppermute | solution.py:26
  48.6 0.0 collective-permute-done.5.product
  48.6 0.4 shard_map.84
  49.1 9.1 %all-gather = f32[16,256]{1,0:T(8,128)S(1)} all-gather(f32[8,256]{1,0:T(8,128)S(1)} %get-tuple-element.41), channel_id=2, replica_groups=mesh['groups'=2,'seq'=16,'head'=8,'dim'=2] {'dim'}, dimensions={0}, use_global_device_ids=true | all-gather | bytes 24576 | tf_op jit(solution)/shard_map/all_gather | solution.py:394
  58.1 0.7 %shard_map.85 = bf16[2,2,64,256]{3,2,1,0:T(8,128)(2,1)} custom-call(f32[2,2,64,256]{3,2,1,0:T(8,128)S(1)} %get-tuple-element.40.raw, f32[2,8,256]{2,1,0:T(8,128)S(1)} %bitcast.7, f32[2,2,64,256]{3,2,1,0:T(8,128)S(1)} %get-tuple-element.42.factor), custom_call_target="tpu_custom_call" | custom-call | tf_op jit(solution)/shard_map/pallas_call | solution.py:305
Async XLA Ops:
  5.8 12.2 %collective-permute-start.4 = (f32[2,2,128,128]{3,2,1,0:T(8,128)S(1)}, f32[2,2,128,128]{3,2,1,0:T(8,128)S(1)}, u32[]{:S(2)}, u32[]{:S(2)}) collective-permute-start(f32[2,2,128,128]{3,2,1,0:T(8,128)S(1)} %get-tuple-element.39), channel_id=1, source_target_pairs={{16,32},{32,48},{48,64},{64,80},{80,96},{96,112},{112,128},{128,14... | collective-permute-start | bytes 786440 | tf_op jit(solution)/shard_map/ppermute | solution.py:26
  11.6 33.8 %collective-permute-start.2 = (f32[2,2,64,128]{3,2,1,0:T(8,128)S(1)}, f32[2,2,64,128]{3,2,1,0:T(8,128)S(1)}, u32[]{:S(2)}, u32[]{:S(2)}) collective-permute-start(f32[2,2,64,128]{3,2,1,0:T(8,128)S(1)} %get-tuple-element.38), channel_id=1, source_target_pairs={{0,48},{1,49},{2,50},{3,51},{4,52},{5,53},{6,54},{7,55},{8,56},{9,... | collective-permute-start | bytes 393224 | tf_op jit(solution)/shard_map/ppermute | solution.py:26
  12.2 14.7 %collective-permute-start = (f32[2,2,64,128]{3,2,1,0:T(8,128)S(1)}, f32[2,2,64,128]{3,2,1,0:T(8,128)S(1)}, u32[]{:S(2)}, u32[]{:S(2)}) collective-permute-start(f32[2,2,64,128]{3,2,1,0:T(8,128)S(1)} %get-tuple-element.38), channel_id=1, source_target_pairs={{0,16},{16,32},{32,48},{48,64},{64,80},{80,96},{96,112},{112,128},... | collective-permute-start | bytes 393224 | tf_op jit(solution)/shard_map/ppermute | solution.py:26
  18.3 30.3 %collective-permute-start.5 = (f32[2,2,128,128]{3,2,1,0:T(8,128)S(1)}, f32[2,2,128,128]{3,2,1,0:T(8,128)S(1)}, u32[]{:S(2)}, u32[]{:S(2)}) collective-permute-start(f32[2,2,128,128]{3,2,1,0:T(8,128)S(1)} %fusion.1), channel_id=1, source_target_pairs={{32,48},{48,64},{64,80},{80,96},{96,112},{112,128},{128,144},{144,... | collective-permute-start | bytes 786440 | tf_op jit(solution)/shard_map/ppermute | solution.py:26
  27.2 18.1 %collective-permute-start.3 = (f32[2,2,64,128]{3,2,1,0:T(8,128)S(1)}, f32[2,2,64,128]{3,2,1,0:T(8,128)S(1)}, u32[]{:S(2)}, u32[]{:S(2)}) collective-permute-start(f32[2,2,64,128]{3,2,1,0:T(8,128)S(1)} %get-tuple-element.43), channel_id=1, source_target_pairs={{16,64},{32,80},{48,96},{64,112},{80,128},{96,144},{112,160},{128,... | collective-permute-start | bytes 393224 | tf_op jit(solution)/shard_map/ppermute | solution.py:26
  38.3 10.3 %collective-permute-start.1 = (f32[2,2,64,128]{3,2,1,0:T(8,128)S(1)}, f32[2,2,64,128]{3,2,1,0:T(8,128)S(1)}, u32[]{:S(2)}, u32[]{:S(2)}) collective-permute-start(f32[2,2,64,128]{3,2,1,0:T(8,128)S(1)} %get-tuple-element.44), channel_id=1, source_target_pairs={{16,32},{32,48},{48,64},{64,80},{80,96},{96,112},{112,128},{128,14... | collective-permute-start | bytes 393224 | tf_op jit(solution)/shard_map/ppermute | solution.py:26
